TPU v7x, 256 devices: a whole 4x4x8 slice. The times are simulated.
256 devices in a mesh: seq: 32 (over y, z_hi, core), head: 8 (over x, z_lo).
Axes of the slice: x: 4, y: 4, z: 8 (z_hi: 4, z_lo: 2; z = z_hi * 2 + z_lo), core: 2. Of those that a mesh axis runs over, the one named last changes fastest.
Arguments:
- queries: bfloat16 [512, 64, 128], P('seq', 'head'), may hold values from -5 to 5
- cache: bfloat16 [2, 2048, 8, 128, 128], P(None, 'seq', 'head'), may hold values from -5 to 5
- page_table: int32 [512, 64], replicated, may hold values from 0 to 2047, as said below
- page_count: int32 [512], replicated, may hold values from 32 to 64, as said below
- out_weight: bfloat16 [8192, 8192], P('head', 'seq'), may hold values from -0.0625 to 0.0625
Outputs:
- output: bfloat16 [512, 8192], P('head', 'seq')
Inputs may be any that keep to these rules, and one draw needn't show every extreme that they name: `page_table`: within a row all 64 entries are distinct page ids; only the first page_count entries of a row are selected, the rest are arbitrary. In every row at most 4 entries lie in one aligned block of 64 page ids, and the first 4 entries of every row lie in one such block. `page_count`: some sequence has exactly 64 selected pages.
All inputs are finite; a program needn't handle non-finite values.
Results may differ from a plain program's by a relative error of at most 0.0095.
Values may be sent and summed in bfloat16 or wider, within the bound.
A program may use at most 128 MiB of HBM per device.

v0:
```python
import math

import jax
import jax.numpy as jnp
from jax import lax
from jax.sharding import PartitionSpec as P

CAP = 4


def passed_along(block, axis, distance):
    devices = range(lax.axis_size(axis))
    route = [((i - distance) % len(devices), i) for i in devices]
    return lax.ppermute(block, axis, route)


def sent_to_all(array, axis):
    copies = jnp.broadcast_to(array, (lax.axis_size(axis), *array.shape))
    return lax.all_to_all(copies, axis, split_axis=0, concat_axis=0, tiled=True)


def in_order(tiles, dim):
    shape = list(tiles.shape[1:])
    shape[dim] *= tiles.shape[0]
    return jnp.moveaxis(tiles, 0, dim).reshape(shape)


def collect(array, axis, dim):
    tiles = sent_to_all(array, axis)
    return in_order(tiles, dim)


def split_up(array, dim, size):
    shape = array.shape
    tiles = array.reshape(*shape[:dim], size, shape[dim] // size, *shape[dim + 1 :])
    return jnp.moveaxis(tiles, dim, 0)


def sum_at_owner(array, axis, dim):
    size = lax.axis_size(axis)
    tiles = lax.all_to_all(split_up(array, dim, size), axis, 0, 0, tiled=True)
    return jnp.sum(tiles, axis=0)


def shards(queries, cache, page_table, page_count, out_weight):
    cycle_size = lax.axis_size("seq")
    own_index = lax.axis_index("seq")
    key_pages = cache[0]
    value_pages = cache[1]
    pages_here = key_pages.shape[0]
    kv_local = key_pages.shape[1]
    query_heads = queries.shape[1]
    head_dim = queries.shape[2]
    group_size = query_heads // kv_local
    score_scale = 1.0 / math.sqrt(head_dim)

    def local_pages(selected, counts):
        slots = selected.shape[1]
        position = jnp.arange(slots, dtype=jnp.int32)
        usable = position[None, :] < counts[:, None]
        present = usable & (selected // pages_here == own_index)
        upper = (position[:, None] <= position[None, :]).astype(jnp.float32)
        ranks = jnp.dot(present.astype(jnp.float32), upper).astype(jnp.int32) - 1
        target = jnp.arange(CAP, dtype=jnp.int32)[None, :, None]
        onehot = present[:, None, :] & (ranks[:, None, :] == target)
        picked = jnp.sum(jnp.where(onehot, selected[:, None, :], 0), axis=2)
        valid = jnp.any(onehot, axis=2)
        index = jnp.where(valid, picked - own_index * pages_here, 0)
        return (index, valid)

    def block_scores(query_block, index, valid):
        block_rows = query_block.shape[0]
        grouped = query_block.reshape(block_rows, kv_local, group_size, head_dim)
        keys = key_pages[index]
        scores = (
            jnp.einsum("skgd,scktd->skgct", grouped, keys, preferred_element_type=jnp.float32)
            * score_scale
        )
        allowed = valid[:, None, None, :, None]
        return jnp.where(allowed, scores, jnp.float32(-1e30))

    def weigh_block(scores, index, valid, maxima):
        allowed = valid[:, None, None, :, None]
        weights = jnp.where(allowed, jnp.exp(scores - maxima[..., None, None]), jnp.float32(0.0))
        totals = jnp.sum(weights, axis=(3, 4))
        values = value_pages[index]
        update = jnp.einsum(
            "skgct,scktd->skgd",
            weights.astype(jnp.bfloat16),
            values,
            preferred_element_type=jnp.float32,
        )
        return (totals, update)

    block_rows = queries.shape[0]

    def visit(turn_index, carry):
        query_block, maxima, totals, outputs = carry
        source = (own_index - turn_index) % cycle_size
        selected = lax.dynamic_slice_in_dim(page_table, source * block_rows, block_rows, 0)
        counts = lax.dynamic_slice_in_dim(page_count, source * block_rows, block_rows, 0)
        index, valid = local_pages(selected, counts)
        scores = block_scores(query_block, index, valid)
        new_maxima = jnp.maximum(maxima, jnp.max(scores, axis=(3, 4)))
        part_totals, update = weigh_block(scores, index, valid, new_maxima)
        rescale = jnp.exp(maxima - new_maxima)
        totals = totals * rescale + part_totals
        outputs = outputs * rescale[..., None] + update
        query_block = passed_along(query_block, "seq", 1)
        new_maxima, totals, outputs = passed_along((new_maxima, totals, outputs), "seq", 1)
        return (query_block, new_maxima, totals, outputs)

    maxima = jnp.full((block_rows, kv_local, group_size), -1e30, jnp.float32)
    totals = jnp.zeros((block_rows, kv_local, group_size), jnp.float32)
    outputs = jnp.zeros((block_rows, kv_local, group_size, head_dim), jnp.float32)
    carried = lax.fori_loop(0, cycle_size, visit, (queries, maxima, totals, outputs))
    finished = (
        (carried[3] / carried[2][..., None])
        .reshape(block_rows, query_heads * head_dim)
        .astype(jnp.bfloat16)
    )
    attention = collect(finished, "seq", 0)
    picked = attention
    summed = sum_at_owner(
        jnp.dot(picked, out_weight, preferred_element_type=jnp.float32), "head", 0
    )
    return summed.astype(jnp.bfloat16)


def solution(mesh):
    return jax.shard_map(
        shards,
        mesh=mesh,
        in_specs=(
            P("seq", "head", None),
            P(None, "seq", "head", None, None),
            P(),
            P(),
            P("head", "seq"),
        ),
        out_specs=P("head", "seq"),
        check_vma=False,
    )
```

profile of v0, /device:TPU:33, one launch (start us, length us, event | category | flops | bytes accessed | tf_op | source)
XLA Modules:
  0.0 580.1 jit_solution(12969125888564356262)
XLA Ops:
  1.1 4.7 slice_bitcast_fusion
  5.9 518.9 %while.22 = (s32[]{:T(128)}, bf16[16,8,128]{2,1,0:T(8,128)(2,1)S(1)}, f32[16,1,8]{0,2,1:T(8,128)S(1)}, f32[16,1,8]{0,2,1:T(8,128)S(1)}, f32[16,1,8,128]{3,2,0,1:...) while((s32[]{:T(128)}, ...), condition=%wide.region_5.6_spmd, body=%wide.region_0.5_spmd.sunk | while | flops 34362960 | bytes 14044788 | solution.py:116
  5.9 3.6 collective-permute-start
  17.6 3.7 collective-permute-start.3
  65.9 3.6 collective-permute-start.3
  82.4 3.7 collective-permute-start.3
  134.9 4.0 collective-permute-start
  212.4 3.6 collective-permute-done.2
  228.6 3.6 collective-permute-done.2
  240.5 4.1 collective-permute-start.3
  258.1 4.5 collective-permute-start.3
  293.7 3.6 collective-permute-done.2
  309.9 3.6 collective-permute-done.2
  326.2 3.6 collective-permute-done.2
  342.4 3.6 collective-permute-done.2
  374.9 3.6 collective-permute-done.2
  391.2 3.6 collective-permute-done.2
  407.4 3.6 collective-permute-done.2
  423.7 3.6 collective-permute-done.2
  439.9 3.6 collective-permute-done.2
  456.2 3.6 collective-permute-done.2
  472.5 3.6 collective-permute-done.2
  525.1 40.6 %all_to_all.10 = bf16[32,16,1024]{2,1,0:T(8,128)(2,1)S(1)} all-to-all(bf16[32,16,1024]{2,1,0:T(8,128)(2,1)S(1)} %broadcast_in_dim.122), channel_id=1, replica_groups=mesh['seq'=32,'head'=8] {'seq'}, dimensions={0} | all-to-all | bytes 2097152 | tf_op jit(solution)/shard_map/all_to_all | solution.py:19
  566.2 13.3 %all_to_all.11 = f32[8,64,256]{2,1,0:T(8,128)S(1)} all-to-all(f32[8,64,256]{2,1,0:T(8,128)S(1)} %fusion.19), channel_id=1, replica_groups=mesh['seq'=32,'head'=8] {'head'}, dimensions={0} | all-to-all | bytes 1048576 | tf_op jit(solution)/shard_map/all_to_all | solution.py:41
  (986 shorter events, 445.5 us)
Async XLA Ops:
  5.9 17.5 %collective-permute-start = (bf16[16,8,128]{2,1,0:T(8,128)(2,1)S(1)}, bf16[16,8,128]{2,1,0:T(8,128)(2,1)S(1)}, u32[]{:S(2)}, u32[]{:S(2)}) collective-permute-start(bf16[16,8,128]{2,1,0:T(8,128)(2,1)S(1)} %copy.69), channel_id=1, source_target_pairs={{248,0},{0,8},{8,16},{16,24},{24,32},{32,40},{40,48},{48,56},{56,6... | collective-permute-start | bytes 98312 | tf_op jit(solution)/shard_map/while/body/eval_jaxpr/ppermute | solution.py:14
  54.3 16.7 %collective-permute-start = (bf16[16,8,128]{2,1,0:T(8,128)(2,1)S(1)}, bf16[16,8,128]{2,1,0:T(8,128)(2,1)S(1)}, u32[]{:S(2)}, u32[]{:S(2)}) collective-permute-start(bf16[16,8,128]{2,1,0:T(8,128)(2,1)S(1)} %copy.69), channel_id=1, source_target_pairs={{248,0},{0,8},{8,16},{16,24},{24,32},{32,40},{40,48},{48,56},{56,6... | collective-permute-start | bytes 98312 | tf_op jit(solution)/shard_map/while/body/eval_jaxpr/ppermute | solution.py:14
  71.0 16.6 %collective-permute-start = (bf16[16,8,128]{2,1,0:T(8,128)(2,1)S(1)}, bf16[16,8,128]{2,1,0:T(8,128)(2,1)S(1)}, u32[]{:S(2)}, u32[]{:S(2)}) collective-permute-start(bf16[16,8,128]{2,1,0:T(8,128)(2,1)S(1)} %copy.69), channel_id=1, source_target_pairs={{248,0},{0,8},{8,16},{16,24},{24,32},{32,40},{40,48},{48,56},{56,6... | collective-permute-start | bytes 98312 | tf_op jit(solution)/shard_map/while/body/eval_jaxpr/ppermute | solution.py:14
  134.9 16.3 %collective-permute-start = (bf16[16,8,128]{2,1,0:T(8,128)(2,1)S(1)}, bf16[16,8,128]{2,1,0:T(8,128)(2,1)S(1)}, u32[]{:S(2)}, u32[]{:S(2)}) collective-permute-start(bf16[16,8,128]{2,1,0:T(8,128)(2,1)S(1)} %copy.69), channel_id=1, source_target_pairs={{248,0},{0,8},{8,16},{16,24},{24,32},{32,40},{40,48},{48,56},{56,6... | collective-permute-start | bytes 98312 | tf_op jit(solution)/shard_map/while/body/eval_jaxpr/ppermute | solution.py:14
  183.5 16.2 %collective-permute-start = (bf16[16,8,128]{2,1,0:T(8,128)(2,1)S(1)}, bf16[16,8,128]{2,1,0:T(8,128)(2,1)S(1)}, u32[]{:S(2)}, u32[]{:S(2)}) collective-permute-start(bf16[16,8,128]{2,1,0:T(8,128)(2,1)S(1)} %copy.69), channel_id=1, source_target_pairs={{248,0},{0,8},{8,16},{16,24},{24,32},{32,40},{40,48},{48,56},{56,6... | collective-permute-start | bytes 98312 | tf_op jit(solution)/shard_map/while/body/eval_jaxpr/ppermute | solution.py:14
  199.7 16.2 %collective-permute-start = (bf16[16,8,128]{2,1,0:T(8,128)(2,1)S(1)}, bf16[16,8,128]{2,1,0:T(8,128)(2,1)S(1)}, u32[]{:S(2)}, u32[]{:S(2)}) collective-permute-start(bf16[16,8,128]{2,1,0:T(8,128)(2,1)S(1)} %copy.69), channel_id=1, source_target_pairs={{248,0},{0,8},{8,16},{16,24},{24,32},{32,40},{40,48},{48,56},{56,6... | collective-permute-start | bytes 98312 | tf_op jit(solution)/shard_map/while/body/eval_jaxpr/ppermute | solution.py:14
  216.0 16.2 %collective-permute-start = (bf16[16,8,128]{2,1,0:T(8,128)(2,1)S(1)}, bf16[16,8,128]{2,1,0:T(8,128)(2,1)S(1)}, u32[]{:S(2)}, u32[]{:S(2)}) collective-permute-start(bf16[16,8,128]{2,1,0:T(8,128)(2,1)S(1)} %copy.69), channel_id=1, source_target_pairs={{248,0},{0,8},{8,16},{16,24},{24,32},{32,40},{40,48},{48,56},{56,6... | collective-permute-start | bytes 98312 | tf_op jit(solution)/shard_map/while/body/eval_jaxpr/ppermute | solution.py:14
  232.2 16.2 %collective-permute-start = (bf16[16,8,128]{2,1,0:T(8,128)(2,1)S(1)}, bf16[16,8,128]{2,1,0:T(8,128)(2,1)S(1)}, u32[]{:S(2)}, u32[]{:S(2)}) collective-permute-start(bf16[16,8,128]{2,1,0:T(8,128)(2,1)S(1)} %copy.69), channel_id=1, source_target_pairs={{248,0},{0,8},{8,16},{16,24},{24,32},{32,40},{40,48},{48,56},{56,6... | collective-permute-start | bytes 98312 | tf_op jit(solution)/shard_map/while/body/eval_jaxpr/ppermute | solution.py:14
  248.5 16.2 %collective-permute-start = (bf16[16,8,128]{2,1,0:T(8,128)(2,1)S(1)}, bf16[16,8,128]{2,1,0:T(8,128)(2,1)S(1)}, u32[]{:S(2)}, u32[]{:S(2)}) collective-permute-start(bf16[16,8,128]{2,1,0:T(8,128)(2,1)S(1)} %copy.69), channel_id=1, source_target_pairs={{248,0},{0,8},{8,16},{16,24},{24,32},{32,40},{40,48},{48,56},{56,6... | collective-permute-start | bytes 98312 | tf_op jit(solution)/shard_map/while/body/eval_jaxpr/ppermute | solution.py:14
  264.7 16.2 %collective-permute-start = (bf16[16,8,128]{2,1,0:T(8,128)(2,1)S(1)}, bf16[16,8,128]{2,1,0:T(8,128)(2,1)S(1)}, u32[]{:S(2)}, u32[]{:S(2)}) collective-permute-start(bf16[16,8,128]{2,1,0:T(8,128)(2,1)S(1)} %copy.69), channel_id=1, source_target_pairs={{248,0},{0,8},{8,16},{16,24},{24,32},{32,40},{40,48},{48,56},{56,6... | collective-permute-start | bytes 98312 | tf_op jit(solution)/shard_map/while/body/eval_jaxpr/ppermute | solution.py:14
  281.0 16.2 %collective-permute-start = (bf16[16,8,128]{2,1,0:T(8,128)(2,1)S(1)}, bf16[16,8,128]{2,1,0:T(8,128)(2,1)S(1)}, u32[]{:S(2)}, u32[]{:S(2)}) collective-permute-start(bf16[16,8,128]{2,1,0:T(8,128)(2,1)S(1)} %copy.69), channel_id=1, source_target_pairs={{248,0},{0,8},{8,16},{16,24},{24,32},{32,40},{40,48},{48,56},{56,6... | collective-permute-start | bytes 98312 | tf_op jit(solution)/shard_map/while/body/eval_jaxpr/ppermute | solution.py:14
  297.2 16.2 %collective-permute-start = (bf16[16,8,128]{2,1,0:T(8,128)(2,1)S(1)}, bf16[16,8,128]{2,1,0:T(8,128)(2,1)S(1)}, u32[]{:S(2)}, u32[]{:S(2)}) collective-permute-start(bf16[16,8,128]{2,1,0:T(8,128)(2,1)S(1)} %copy.69), channel_id=1, source_target_pairs={{248,0},{0,8},{8,16},{16,24},{24,32},{32,40},{40,48},{48,56},{56,6... | collective-permute-start | bytes 98312 | tf_op jit(solution)/shard_map/while/body/eval_jaxpr/ppermute | solution.py:14
  313.5 16.2 %collective-permute-start = (bf16[16,8,128]{2,1,0:T(8,128)(2,1)S(1)}, bf16[16,8,128]{2,1,0:T(8,128)(2,1)S(1)}, u32[]{:S(2)}, u32[]{:S(2)}) collective-permute-start(bf16[16,8,128]{2,1,0:T(8,128)(2,1)S(1)} %copy.69), channel_id=1, source_target_pairs={{248,0},{0,8},{8,16},{16,24},{24,32},{32,40},{40,48},{48,56},{56,6... | collective-permute-start | bytes 98312 | tf_op jit(solution)/shard_map/while/body/eval_jaxpr/ppermute | solution.py:14
  329.7 16.2 %collective-permute-start = (bf16[16,8,128]{2,1,0:T(8,128)(2,1)S(1)}, bf16[16,8,128]{2,1,0:T(8,128)(2,1)S(1)}, u32[]{:S(2)}, u32[]{:S(2)}) collective-permute-start(bf16[16,8,128]{2,1,0:T(8,128)(2,1)S(1)} %copy.69), channel_id=1, source_target_pairs={{248,0},{0,8},{8,16},{16,24},{24,32},{32,40},{40,48},{48,56},{56,6... | collective-permute-start | bytes 98312 | tf_op jit(solution)/shard_map/while/body/eval_jaxpr/ppermute | solution.py:14
  346.0 16.2 %collective-permute-start = (bf16[16,8,128]{2,1,0:T(8,128)(2,1)S(1)}, bf16[16,8,128]{2,1,0:T(8,128)(2,1)S(1)}, u32[]{:S(2)}, u32[]{:S(2)}) collective-permute-start(bf16[16,8,128]{2,1,0:T(8,128)(2,1)S(1)} %copy.69), channel_id=1, source_target_pairs={{248,0},{0,8},{8,16},{16,24},{24,32},{32,40},{40,48},{48,56},{56,6... | collective-permute-start | bytes 98312 | tf_op jit(solution)/shard_map/while/body/eval_jaxpr/ppermute | solution.py:14
  362.3 16.2 %collective-permute-start = (bf16[16,8,128]{2,1,0:T(8,128)(2,1)S(1)}, bf16[16,8,128]{2,1,0:T(8,128)(2,1)S(1)}, u32[]{:S(2)}, u32[]{:S(2)}) collective-permute-start(bf16[16,8,128]{2,1,0:T(8,128)(2,1)S(1)} %copy.69), channel_id=1, source_target_pairs={{248,0},{0,8},{8,16},{16,24},{24,32},{32,40},{40,48},{48,56},{56,6... | collective-permute-start | bytes 98312 | tf_op jit(solution)/shard_map/while/body/eval_jaxpr/ppermute | solution.py:14
  378.5 16.2 %collective-permute-start = (bf16[16,8,128]{2,1,0:T(8,128)(2,1)S(1)}, bf16[16,8,128]{2,1,0:T(8,128)(2,1)S(1)}, u32[]{:S(2)}, u32[]{:S(2)}) collective-permute-start(bf16[16,8,128]{2,1,0:T(8,128)(2,1)S(1)} %copy.69), channel_id=1, source_target_pairs={{248,0},{0,8},{8,16},{16,24},{24,32},{32,40},{40,48},{48,56},{56,6... | collective-permute-start | bytes 98312 | tf_op jit(solution)/shard_map/while/body/eval_jaxpr/ppermute | solution.py:14
  394.8 16.2 %collective-permute-start = (bf16[16,8,128]{2,1,0:T(8,128)(2,1)S(1)}, bf16[16,8,128]{2,1,0:T(8,128)(2,1)S(1)}, u32[]{:S(2)}, u32[]{:S(2)}) collective-permute-start(bf16[16,8,128]{2,1,0:T(8,128)(2,1)S(1)} %copy.69), channel_id=1, source_target_pairs={{248,0},{0,8},{8,16},{16,24},{24,32},{32,40},{40,48},{48,56},{56,6... | collective-permute-start | bytes 98312 | tf_op jit(solution)/shard_map/while/body/eval_jaxpr/ppermute | solution.py:14
  411.0 16.2 %collective-permute-start = (bf16[16,8,128]{2,1,0:T(8,128)(2,1)S(1)}, bf16[16,8,128]{2,1,0:T(8,128)(2,1)S(1)}, u32[]{:S(2)}, u32[]{:S(2)}) collective-permute-start(bf16[16,8,128]{2,1,0:T(8,128)(2,1)S(1)} %copy.69), channel_id=1, source_target_pairs={{248,0},{0,8},{8,16},{16,24},{24,32},{32,40},{40,48},{48,56},{56,6... | collective-permute-start | bytes 98312 | tf_op jit(solution)/shard_map/while/body/eval_jaxpr/ppermute | solution.py:14
  427.3 16.2 %collective-permute-start = (bf16[16,8,128]{2,1,0:T(8,128)(2,1)S(1)}, bf16[16,8,128]{2,1,0:T(8,128)(2,1)S(1)}, u32[]{:S(2)}, u32[]{:S(2)}) collective-permute-start(bf16[16,8,128]{2,1,0:T(8,128)(2,1)S(1)} %copy.69), channel_id=1, source_target_pairs={{248,0},{0,8},{8,16},{16,24},{24,32},{32,40},{40,48},{48,56},{56,6... | collective-permute-start | bytes 98312 | tf_op jit(solution)/shard_map/while/body/eval_jaxpr/ppermute | solution.py:14
  443.5 16.2 %collective-permute-start = (bf16[16,8,128]{2,1,0:T(8,128)(2,1)S(1)}, bf16[16,8,128]{2,1,0:T(8,128)(2,1)S(1)}, u32[]{:S(2)}, u32[]{:S(2)}) collective-permute-start(bf16[16,8,128]{2,1,0:T(8,128)(2,1)S(1)} %copy.69), channel_id=1, source_target_pairs={{248,0},{0,8},{8,16},{16,24},{24,32},{32,40},{40,48},{48,56},{56,6... | collective-permute-start | bytes 98312 | tf_op jit(solution)/shard_map/while/body/eval_jaxpr/ppermute | solution.py:14
  459.8 16.2 %collective-permute-start = (bf16[16,8,128]{2,1,0:T(8,128)(2,1)S(1)}, bf16[16,8,128]{2,1,0:T(8,128)(2,1)S(1)}, u32[]{:S(2)}, u32[]{:S(2)}) collective-permute-start(bf16[16,8,128]{2,1,0:T(8,128)(2,1)S(1)} %copy.69), channel_id=1, source_target_pairs={{248,0},{0,8},{8,16},{16,24},{24,32},{32,40},{40,48},{48,56},{56,6... | collective-permute-start | bytes 98312 | tf_op jit(solution)/shard_map/while/body/eval_jaxpr/ppermute | solution.py:14
  476.0 16.2 %collective-permute-start = (bf16[16,8,128]{2,1,0:T(8,128)(2,1)S(1)}, bf16[16,8,128]{2,1,0:T(8,128)(2,1)S(1)}, u32[]{:S(2)}, u32[]{:S(2)}) collective-permute-start(bf16[16,8,128]{2,1,0:T(8,128)(2,1)S(1)} %copy.69), channel_id=1, source_target_pairs={{248,0},{0,8},{8,16},{16,24},{24,32},{32,40},{40,48},{48,56},{56,6... | collective-permute-start | bytes 98312 | tf_op jit(solution)/shard_map/while/body/eval_jaxpr/ppermute | solution.py:14
  492.3 16.2 %collective-permute-start = (bf16[16,8,128]{2,1,0:T(8,128)(2,1)S(1)}, bf16[16,8,128]{2,1,0:T(8,128)(2,1)S(1)}, u32[]{:S(2)}, u32[]{:S(2)}) collective-permute-start(bf16[16,8,128]{2,1,0:T(8,128)(2,1)S(1)} %copy.69), channel_id=1, source_target_pairs={{248,0},{0,8},{8,16},{16,24},{24,32},{32,40},{40,48},{48,56},{56,6... | collective-permute-start | bytes 98312 | tf_op jit(solution)/shard_map/while/body/eval_jaxpr/ppermute | solution.py:14
  (106 other events, 1243.8 us)
where the time goes:
time: 585 us; the launch traced here: 580 us
  local copies, waits for them, and re-layouts  211 us (36%)
  starting transfers between devices  143 us (24%)
  waiting for transfers between devices  107 us (18%)
  blocking collectives  53.9 us (9%)
  matrix products  42 us (7%)
  other arithmetic  21.2 us (4%)
    ppermute x128, starting transfers between devices, passed_along(): return lax.ppermute(block, axis, route)  143 us
    ppermute x128, waiting for transfers between devices, passed_along(): return lax.ppermute(block, axis, route)  107 us
    gather x32, local copies, waits for them, and re-layouts, block_scores(): keys = key_pages[index]  81.3 us
    gather x32, local copies, waits for them, and re-layouts, weigh_block(): values = value_pages[index]  81.3 us
    all_to_all x1, blocking collectives, sent_to_all(): return lax.all_to_all(copies, axis, split_axis=0, concat_axis=0, tiled=True)  40.6 us
    dynamic_slice x32, local copies, waits for them, and re-layouts, visit(): lax.dynamic_slice_in_dim(page_count, source * block_rows, block_rows, 0)  24.2 us
    dot_general x32, matrix products, block_scores(): jnp.einsum('skgd,scktd->skgct', grouped, keys, preferred_element_type=jnp...  23.3 us
    dot_general x32, matrix products, weigh_block(): jnp.einsum('skgct,scktd->skgd', weights.astype(jnp.bfloat16), values, pre...  14 us
  transfers between devices with their start and end apart: 128, of which 49 were waited for; matrix products, arithmetic and copies ran while one was open for 46% of the time, Pallas kernels for 0%

commit v1 on v0

v1 whole, which is shorter than its diff:
```python
import functools
import math

import jax
import jax.numpy as jnp
from jax import lax
from jax.experimental import pallas as pl
from jax.experimental.pallas import tpu as pltpu
from jax.sharding import PartitionSpec as P

Y, Z, C = 4, 4, 2
BLOCKS = Y * Z * C
ROWS = 16
HEADS = 8
HD = 128
PAGE = 128
PAGES = 64
SLOTS = 64
BATCH = BLOCKS * ROWS
TILE = ROWS * HEADS
GROUPS = 8
LOWEST = -1024.0
LOG2E_SCALE = math.log2(math.e) / math.sqrt(HD)
F32, BF16 = jnp.float32, jnp.bfloat16
VMEM = pltpu.VMEM


def position():
    me = lax.axis_index("seq")
    return me // (Z * C), (me // C) % Z, me % C


def at_seq(y, z, c):
    return {"seq": (y * Z + z) * C + c}


def send(src, dst, send_sem, recv_sem, device):
    copy = pltpu.make_async_remote_copy(
        src_ref=src, dst_ref=dst, send_sem=send_sem, recv_sem=recv_sem,
        device_id=device, device_id_type=pl.DeviceIdType.MESH,
    )
    copy.start()
    return copy


def arrived(dst, send_sem, recv_sem, device):
    pltpu.make_async_remote_copy(
        src_ref=dst, dst_ref=dst, send_sem=send_sem, recv_sem=recv_sem,
        device_id=device, device_id_type=pl.DeviceIdType.MESH,
    ).wait_recv()


def seq_peers(y, z, c):
    peers = [at_seq(y, z, 1 - c)]
    peers += [at_seq(y, (z + d) % Z, c) for d in range(1, Z)]
    peers += [at_seq((y + d) % Y, z, c) for d in range(1, Y)]
    return peers


def greet(peers):
    barrier = pltpu.get_barrier_semaphore()
    for peer in peers:
        pl.semaphore_signal(barrier, inc=1, device_id=peer, device_id_type=pl.DeviceIdType.MESH)
    pl.semaphore_wait(barrier, len(peers))


class Gather:
    def __init__(self, buf, zs, zr, ys, yr, ds, dr):
        self.buf, self.sems = buf, (zs, zr, ys, yr, ds, dr)
        self.y, self.z, self.c = position()
        self.copies = []

    def spread(self, dz):
        y, z, c = self.y, self.z, self.c
        zs, zr, ys, yr, ds, dr = self.sems
        block = self.buf.at[y, (z - dz + Z) % Z, c]
        for dy in (2, 1, 3):
            self.copies.append(send(block, block, ys.at[dy, dz], yr.at[dy, dz], at_seq((y + dy) % Y, z, c)))
        self.copies.append(send(block, block, ds.at[0, dz], dr.at[0, dz], at_seq(y, z, 1 - c)))

    def start(self):
        y, z, c = self.y, self.z, self.c
        zs, zr, ys, yr, ds, dr = self.sems
        own = self.buf.at[y, z, c]
        for dz in (2, 1, 3):
            self.copies.append(send(own, own, zs.at[dz], zr.at[dz], at_seq(y, (z + dz) % Z, c)))
        self.spread(0)

    def from_z(self, dz):
        y, z, c = self.y, self.z, self.c
        zs, zr, ys, yr, ds, dr = self.sems
        arrived(self.buf.at[y, (z - dz + Z) % Z, c], zs.at[dz], zr.at[dz], at_seq(y, (z - dz + Z) % Z, c))
        self.spread(dz)

    def from_y(self, dy, dz):
        y, z, c = self.y, self.z, self.c
        zs, zr, ys, yr, ds, dr = self.sems
        block = self.buf.at[(y - dy + Y) % Y, (z - dz + Z) % Z, c]
        arrived(block, ys.at[dy, dz], yr.at[dy, dz], at_seq((y - dy + Y) % Y, z, c))
        self.copies.append(send(block, block, ds.at[dy, dz], dr.at[dy, dz], at_seq(y, z, 1 - c)))

    def from_core(self, dy, dz):
        y, z, c = self.y, self.z, self.c
        zs, zr, ys, yr, ds, dr = self.sems
        block = self.buf.at[(y - dy + Y) % Y, (z - dz + Z) % Z, 1 - c]
        arrived(block, ds.at[dy, dz], dr.at[dy, dz], at_seq(y, z, 1 - c))

    def finish(self):
        for copy in self.copies:
            copy.wait_send()


ORDER = [(0, 0)] + [(0, d) for d in (1, 3, 2)] + [(dy, dz) for dz in (0, 1, 3, 2) for dy in (1, 3, 2)]
GATHER_SEMS = [
    pltpu.SemaphoreType.DMA((Z,)), pltpu.SemaphoreType.DMA((Z,)),
    pltpu.SemaphoreType.DMA((Y, Z)), pltpu.SemaphoreType.DMA((Y, Z)),
    pltpu.SemaphoreType.DMA((Y, Z)), pltpu.SemaphoreType.DMA((Y, Z)),
]


def dot(a, b, dims=((1,), (0,))):
    return lax.dot_general(a, b, (dims, ((), ())), preferred_element_type=F32)


def selection(table, counts):
    own = lax.axis_index("seq")
    square = lambda n, f: f(lax.broadcasted_iota(jnp.int32, (n, n), 0), lax.broadcasted_iota(jnp.int32, (n, n), 1)).astype(F32).astype(BF16)
    eye = square(SLOTS, jnp.equal)
    block = dot(eye, (table // PAGES).astype(F32).astype(BF16), ((1,), (1,)))
    page = dot(eye, (table % PAGES).astype(F32).astype(BF16), ((1,), (1,)))
    slot = lax.broadcasted_iota(jnp.int32, (SLOTS, BATCH), 0)
    present = (slot < counts) & (block == own.astype(F32))
    rank = dot(square(SLOTS, jnp.greater_equal), present.astype(F32).astype(BF16))
    rows = [jnp.sum(jnp.where(present & (rank == k + 1.0), page + 1.0, 0.0), axis=0, keepdims=True) for k in range(4)]
    more = (rows[2] > 0.0).astype(F32)
    place = dot(jnp.broadcast_to(more, (8, BATCH)).astype(BF16), square(BATCH, jnp.less_equal))[0:1]
    total = jnp.sum(more, axis=1, keepdims=True)
    at = lax.broadcasted_iota(jnp.int32, (BATCH, BATCH), 0).astype(F32)
    onehot = jnp.where((at + 1.0 == place) & (more > 0.0), 1.0, 0.0).astype(BF16)
    who = lax.broadcasted_iota(jnp.int32, (8, BATCH), 1)
    high = dot((who // 16).astype(F32).astype(BF16), onehot, ((1,), (1,)))[0:1]
    low = dot((who % 16).astype(F32).astype(BF16), onehot, ((1,), (1,)))[0:1]
    number = lax.broadcasted_iota(jnp.int32, (1, BATCH), 1).astype(F32)
    many = jnp.where(number < total, high * 16.0 + low, float(BATCH))
    return jnp.concatenate(rows + [many, jnp.broadcast_to(total, (1, BATCH))] + [jnp.zeros((2, BATCH), F32)], axis=0).astype(jnp.int32)


def prepare_kernel(q_ref, table_ref, counts_ref, cache_ref, all_ref, pick_ref, kt_ref, keys, turned, key_sems, out_sem, *sems):
    y, z, c = position()
    quarter = PAGES // 4
    loads = [
        pltpu.make_async_copy(cache_ref.at[0, pl.ds(i * quarter, quarter)], keys.at[pl.ds(i * quarter, quarter)], key_sems.at[i])
        for i in range(4)
    ]
    for load in loads:
        load.start()
    greet(seq_peers(y, z, c))
    all_ref[y, z, c] = q_ref[...]
    gather = Gather(all_ref, *sems)
    gather.start()
    pick_ref[...] = selection(table_ref[...], counts_ref[...])

    def turn(i, carry):
        for j in range(4):
            turned[i * 4 + j] = keys[i * 4 + j].T
        return carry

    loads[0].wait()
    loads[1].wait()
    lax.fori_loop(0, 8, turn, 0)
    for dz in (1, 3, 2):
        gather.from_z(dz)
    loads[2].wait()
    loads[3].wait()
    lax.fori_loop(8, 16, turn, 0)
    out = pltpu.make_async_copy(turned, kt_ref, out_sem)
    out.start()
    for dy, dz in ORDER[4:]:
        gather.from_y(dy, dz)
    for dy, dz in ORDER:
        gather.from_core(dy, dz)
    gather.finish()
    out.wait()


def prepare(q, table, counts, cache):
    vmem = pl.BlockSpec(memory_space=VMEM)
    return pl.pallas_call(
        prepare_kernel,
        out_shape=(
            jax.ShapeDtypeStruct((Y, Z, C, TILE, HD), BF16),
            jax.ShapeDtypeStruct((8, BATCH), jnp.int32),
            jax.ShapeDtypeStruct((PAGES, HD, PAGE), BF16),
        ),
        in_specs=[vmem, vmem, vmem, pl.BlockSpec(memory_space=pl.ANY)],
        out_specs=(vmem, vmem, pl.BlockSpec(memory_space=pl.ANY)),
        scratch_shapes=[
            VMEM((PAGES, PAGE, HD), BF16),
            VMEM((PAGES, HD, PAGE), BF16),
            pltpu.SemaphoreType.DMA((4,)),
            pltpu.SemaphoreType.DMA,
            *GATHER_SEMS,
        ],
        compiler_params=pltpu.CompilerParams(collective_id=0, has_side_effects=True, vmem_limit_bytes=32 << 20),
        name="prepare",
    )(q, table, counts, cache)


def attend_kernel(pick, q_in, kt_in, cache_ref, acc_out, stats_out, kt, v, q, scores, acc, top, total, kt_sem, v_sem):
    load_kt = pltpu.make_async_copy(kt_in, kt, kt_sem)
    load_v = pltpu.make_async_copy(cache_ref.at[1], v, v_sem)
    load_kt.start()
    load_v.start()

    def widen(i, carry):
        for j in range(4):
            q[pl.ds((i * 4 + j) * ROWS, ROWS)] = q_in[i * 4 + j].astype(F32).reshape(ROWS, HEADS, HD)
        return carry

    lax.fori_loop(0, BLOCKS // 4, widen, 0)
    q[pl.ds(BATCH, 8)] = jnp.zeros((8, HEADS, HD), F32)
    load_kt.wait()
    zeros = jnp.zeros((HEADS, HD), F32)

    def pages_of(b, first):
        safe = jnp.minimum(b, BATCH - 1)
        picks = [pick[first, safe], pick[first + 1, safe]]
        return [jnp.maximum(p - 1, 0) for p in picks], [jnp.where(p > 0, 0.0, -1e30).astype(F32) for p in picks]

    def score(a, b, first):
        pa, _ = pages_of(a, first)
        pb, _ = pages_of(b, first)
        left = jnp.concatenate(
            [jnp.concatenate([q[a], zeros], axis=1), jnp.concatenate([zeros, q[b]], axis=1)], axis=0
        ).astype(BF16)
        right = jnp.concatenate(
            [jnp.concatenate([kt[pa[0]], kt[pa[1]]], axis=1), jnp.concatenate([kt[pb[0]], kt[pb[1]]], axis=1)], axis=0
        )
        return dot(left, right)

    def weigh(s, b, first):
        _, bias = pages_of(b, first)
        s0 = s[:, :PAGE] * LOG2E_SCALE + bias[0]
        s1 = s[:, PAGE:] * LOG2E_SCALE + bias[1]
        highest = jnp.max(jnp.maximum(s0, s1), axis=1, keepdims=True)
        m = jnp.maximum(jnp.floor(highest * 0.5 + 0.5) * 2.0, LOWEST)
        w0, w1 = jnp.exp2(s0 - m), jnp.exp2(s1 - m)
        return m, jnp.sum(w0 + w1, axis=1, keepdims=True), jnp.concatenate([w0, w1], axis=1)

    def attend(s, a, b, first):
        pa, _ = pages_of(a, first)
        pb, _ = pages_of(b, first)
        ma, la, wa = weigh(s[:HEADS], a, first)
        mb, lb, wb = weigh(s[HEADS:], b, first)
        weights = jnp.concatenate([wa, wb], axis=0).astype(BF16)
        right = jnp.concatenate(
            [jnp.concatenate([v[pa[0]], v[pb[0]]], axis=1), jnp.concatenate([v[pa[1]], v[pb[1]]], axis=1)], axis=0
        )
        o = dot(weights, right)
        return (ma, la, o[:HEADS, :HD]), (mb, lb, o[HEADS:, HD:])

    units = ROWS // 2

    def scores_of(g):
        for u in range(units):
            b = g * ROWS + 2 * u
            scores[u] = score(b, b + 1, 0)

    scores_of(0)
    load_v.wait()

    def step(g, carry):
        for u in range(units):
            b = g * ROWS + 2 * u
            for k, (m, l, o) in enumerate(attend(scores[u], b, b + 1, 0)):
                acc[b + k] = o
                top[b + k] = jnp.broadcast_to(m, (HEADS, HD))
                total[b + k] = jnp.broadcast_to(l, (HEADS, HD))
        scores_of(jnp.minimum(g + 1, BLOCKS - 1))
        return carry

    lax.fori_loop(0, BLOCKS, step, 0)
    many = pick[5, 0]

    def more(i, carry):
        whose = [pick[4, i * ROWS + j] for j in range(ROWS)]
        for u in range(units):
            a, b = whose[2 * u], whose[2 * u + 1]
            for who, (m, l, o) in zip((a, b), attend(score(a, b, 2), a, b, 2)):
                m0 = top[who]
                m1 = jnp.maximum(m0, m)
                f0, f1 = jnp.exp2(m0 - m1), jnp.exp2(m - m1)
                acc[who] = acc[who] * f0 + o * f1
                total[who] = total[who] * f0 + l * f1
                top[who] = m1
        return carry

    lax.fori_loop(0, (many + ROWS - 1) // ROWS, more, 0)
    sublane = lax.broadcasted_iota(jnp.int32, (HEADS, HD), 0)
    lane = lax.broadcasted_iota(jnp.int32, (HEADS, HD), 1)

    def close(g, carry):
        tops = jnp.zeros((HEADS, HD), F32)
        totals = jnp.zeros((HEADS, HD), F32)
        for s in range(ROWS):
            here = lane - sublane == s * HEADS
            tops = jnp.where(here, top[g * ROWS + s], tops)
            totals = jnp.where(here, total[g * ROWS + s], totals)
        stats_out[g, 0:1] = jnp.sum(tops, axis=0, keepdims=True)
        stats_out[g, 1:2] = jnp.sum(totals, axis=0, keepdims=True)
        acc_out[g] = acc[pl.ds(g * ROWS, ROWS)].reshape(TILE, HD).astype(BF16)
        return carry

    lax.fori_loop(0, BLOCKS, close, 0)


def attend(pick, q, kt, cache):
    vmem = pl.BlockSpec(memory_space=VMEM)
    hbm = pl.BlockSpec(memory_space=pl.ANY)
    return pl.pallas_call(
        attend_kernel,
        out_shape=(
            jax.ShapeDtypeStruct((BLOCKS, TILE, HD), BF16),
            jax.ShapeDtypeStruct((BLOCKS, 2, HD), F32),
        ),
        in_specs=[pl.BlockSpec(memory_space=pltpu.SMEM), vmem, hbm, hbm],
        out_specs=(vmem, vmem),
        scratch_shapes=[
            VMEM((PAGES, HD, PAGE), BF16),
            VMEM((PAGES, PAGE, HD), BF16),
            VMEM((BATCH + 8, HEADS, HD), F32),
            VMEM((ROWS // 2, 2 * HEADS, 2 * PAGE), F32),
            VMEM((BATCH + 8, HEADS, HD), F32),
            VMEM((BATCH + 8, HEADS, HD), F32),
            VMEM((BATCH + 8, HEADS, HD), F32),
            pltpu.SemaphoreType.DMA,
            pltpu.SemaphoreType.DMA,
        ],
        compiler_params=pltpu.CompilerParams(vmem_limit_bytes=40 << 20),
        name="attend",
    )(pick, q, kt, cache)


def merge(parts, stats, diagonal):
    m = functools.reduce(jnp.maximum, [s[0:1] for s in stats])
    factors = [jnp.exp2(s[0:1] - m) for s in stats]
    total = sum(s[1:2] * f for s, f in zip(stats, factors))
    left = jnp.concatenate([jnp.where(diagonal, jnp.broadcast_to(f, (TILE, TILE)), 0.0).astype(BF16) for f in factors], axis=1)
    return dot(left, jnp.concatenate(parts, axis=0)), m, total


def finish_kernel(
    acc, stats, w_ref, out_ref,
    core_acc, core_stats, y_out, y_out_stats, y_in, y_in_stats, z_out, z_out_stats, z_in, z_in_stats,
    turned, att, w, part, parts_in, w_sem,
    c_send, c_recv, cs_send, cs_recv, y_send, y_recv, ys_send, ys_recv, z_send, z_recv, zs_send, zs_recv, h_send, h_recv, *sems,
):
    y, z, c = position()
    h = lax.axis_index("head")
    other = 1 - c
    load_w = pltpu.make_async_copy(w_ref, w, w_sem)
    load_w.start()
    greet(seq_peers(y, z, c) + [{"head": (h + d) % GROUPS} for d in range(1, GROUPS)])
    copies = []
    partner = at_seq(y, z, other)
    yorder = (2, 1, 3, 0)
    for d in yorder:
        yy = (y + d) % Y
        copies.append(send(acc.at[yy, :, other], core_acc.at[yy], c_send.at[d], c_recv.at[d], partner))
        copies.append(send(stats.at[yy, :, other], core_stats.at[yy], cs_send.at[d], cs_recv.at[d], partner))
    diagonal = lax.broadcasted_iota(jnp.int32, (TILE, TILE), 0) == lax.broadcasted_iota(jnp.int32, (TILE, TILE), 1)

    for d in yorder:
        yy = (y + d) % Y
        arrived(core_acc.at[yy], c_send.at[d], c_recv.at[d], partner)
        arrived(core_stats.at[yy], cs_send.at[d], cs_recv.at[d], partner)
        for i in range(Z):
            o, m, total = merge([acc[yy, i, c], core_acc[yy, i]], [stats[yy, i, c], core_stats[yy, i]], diagonal)
            if d == 0:
                y_in[0, i] = o.astype(BF16)
                y_in_stats[0, i, 0:1] = m
                y_in_stats[0, i, 1:2] = total
            else:
                y_out[d, i] = o.astype(BF16)
                y_out_stats[d, i, 0:1] = m
                y_out_stats[d, i, 1:2] = total
        if d != 0:
            there = at_seq(yy, z, c)
            copies.append(send(y_out.at[d], y_in.at[d], y_send.at[d], y_recv.at[d], there))
            copies.append(send(y_out_stats.at[d], y_in_stats.at[d], ys_send.at[d], ys_recv.at[d], there))
    for d in (1, 3, 2):
        there = at_seq((y - d + Y) % Y, z, c)
        arrived(y_in.at[d], y_send.at[d], y_recv.at[d], there)
        arrived(y_in_stats.at[d], ys_send.at[d], ys_recv.at[d], there)
    for d in (2, 1, 3, 0):
        zz = (z + d) % Z
        o, m, total = merge([y_in[i, zz] for i in range(Y)], [y_in_stats[i, zz] for i in range(Y)], diagonal)
        if d == 0:
            z_in[0] = o.astype(BF16)
            z_in_stats[0, 0:1] = m
            z_in_stats[0, 1:2] = total
        else:
            z_out[d] = o.astype(BF16)
            z_out_stats[d, 0:1] = m
            z_out_stats[d, 1:2] = total
            there = at_seq(y, zz, c)
            copies.append(send(z_out.at[d], z_in.at[d], z_send.at[d], z_recv.at[d], there))
            copies.append(send(z_out_stats.at[d], z_in_stats.at[d], zs_send.at[d], zs_recv.at[d], there))
    for d in (1, 3, 2):
        there = at_seq(y, (z - d + Z) % Z, c)
        arrived(z_in.at[d], z_send.at[d], z_recv.at[d], there)
        arrived(z_in_stats.at[d], zs_send.at[d], zs_recv.at[d], there)
    o, m, total = merge([z_in[i] for i in range(Z)], [z_in_stats[i] for i in range(Z)], diagonal)
    turned[...] = o / jnp.broadcast_to(total, (TILE, TILE)).T
    for i in range(HEADS):
        att[y, z, c, :, i * HD : (i + 1) * HD] = turned[pl.ds(i, ROWS, stride=HEADS), :].astype(BF16)
    gather = Gather(att, *sems)
    gather.start()
    for dz in (1, 3, 2):
        gather.from_z(dz)
    for dy, dz in ORDER[4:]:
        gather.from_y(dy, dz)
    for dy, dz in ORDER:
        gather.from_core(dy, dz)
    load_w.wait()
    for d in (4, 2, 6, 3, 5, 1, 7, 0):
        hh = (h + d) % GROUPS
        rows = jnp.concatenate([att[hh // 2, (hh % 2) * 2 + i, j] for i in range(2) for j in range(C)], axis=0)
        share = dot(rows, w[...]).astype(BF16)
        if d == 0:
            parts_in[0] = share
        else:
            part[d] = share
            copies.append(send(part.at[d], parts_in.at[d], h_send.at[d], h_recv.at[d], {"head": hh}))
    for d in (1, 7, 2, 6, 3, 5, 4):
        arrived(parts_in.at[d], h_send.at[d], h_recv.at[d], {"head": (h - d + GROUPS) % GROUPS})
    out_ref[...] = sum(parts_in[d].astype(F32) for d in range(GROUPS)).astype(BF16)
    gather.finish()
    for copy in copies:
        copy.wait_send()


def finish(acc, stats, w):
    vmem = pl.BlockSpec(memory_space=VMEM)
    width = w.shape[1]
    rows = BATCH // GROUPS
    dma = pltpu.SemaphoreType.DMA
    return pl.pallas_call(
        finish_kernel,
        out_shape=jax.ShapeDtypeStruct((rows, width), BF16),
        in_specs=[vmem, vmem, pl.BlockSpec(memory_space=pl.ANY)],
        out_specs=vmem,
        scratch_shapes=[
            VMEM((Y, Z, TILE, HD), BF16), VMEM((Y, Z, 2, HD), F32),
            VMEM((Y, Z, TILE, HD), BF16), VMEM((Y, Z, 2, HD), F32),
            VMEM((Y, Z, TILE, HD), BF16), VMEM((Y, Z, 2, HD), F32),
            VMEM((Z, TILE, HD), BF16), VMEM((Z, 2, HD), F32),
            VMEM((Z, TILE, HD), BF16), VMEM((Z, 2, HD), F32),
            VMEM((TILE, HD), F32),
            VMEM((Y, Z, C, ROWS, HEADS * HD), BF16),
            VMEM((HEADS * HD, width), BF16),
            VMEM((GROUPS, rows, width), BF16), VMEM((GROUPS, rows, width), BF16),
            dma,
            *[dma((Y,)) for _ in range(12)],
            dma((GROUPS,)), dma((GROUPS,)),
            *GATHER_SEMS,
        ],
        compiler_params=pltpu.CompilerParams(collective_id=1, has_side_effects=True, vmem_limit_bytes=32 << 20),
        name="finish",
    )(acc, stats, w)


def shards(queries, cache, page_table, page_count, out_weight):
    cache = cache.reshape(2, PAGES, PAGE, HD)
    q, pick, kt = prepare(queries.reshape(TILE, HD), page_table, page_count.reshape(1, BATCH), cache)
    acc, stats = attend(pick, q.reshape(BLOCKS, TILE, HD), kt, cache)
    return finish(acc.reshape(Y, Z, C, TILE, HD), stats.reshape(Y, Z, C, 2, HD), out_weight)


def solution(mesh):
    return jax.shard_map(
        shards,
        mesh=mesh,
        in_specs=(
            P("seq", "head", None),
            P(None, "seq", "head", None, None),
            P(),
            P(),
            P("head", "seq"),
        ),
        out_specs=P("head", "seq"),
        check_vma=False,
    )
```

time: 585 us -> 86 us (0.15)
  local copies, waits for them, and re-layouts: 211 us -> 5.28 us
  starting transfers between devices: 143 us -> 0 us
  waiting for transfers between devices: 107 us -> 0 us
  Pallas kernels: 0 us -> 79.1 us
  blocking collectives: 53.9 us -> 0 us
  matrix products: 42 us -> 0 us
  other arithmetic: 21.2 us -> 0 us
    gather x64 -> x0, local copies, waits for them, and re-layouts: 163 us -> none  [the longest x32 81.3 us: block_scores(): keys = key_pages[index]]
    ppermute x128 -> x0, starting transfers between devices: 143 us -> none  [passed_along(): return lax.ppermute(block, axis, route)]
    ppermute x128 -> x0, waiting for transfers between devices: 107 us -> none  [passed_along(): return lax.ppermute(block, axis, route)]
    pallas_call x0 -> x3, Pallas kernels: none -> 79.1 us  [the longest x1 38.4 us: finish(): pl.pallas_call(finish_kernel, out_shape=jax.ShapeDtypeStruct((rows, width...]
    all_to_all x2 -> x0, blocking collectives: 53.9 us -> none  [the longest x1 40.6 us: sent_to_all(): return lax.all_to_all(copies, axis, split_axis=0, concat_axis=0, tiled=True)]
    dot_general x97 -> x0, matrix products: 42 us -> none  [the longest x32 23.3 us: block_scores(): jnp.einsum('skgd,scktd->skgct', grouped, keys, preferred_element_type=jnp...]
    dynamic_slice x32 -> x0, local copies, waits for them, and re-layouts: 24.2 us -> none  [visit(): lax.dynamic_slice_in_dim(page_count, source * block_rows, block_rows, 0)]
    reduce_sum x65 -> x0, other arithmetic: 12.8 us -> none  [the longest x32 7.26 us: weigh_block(): totals = jnp.sum(weights, axis=(3, 4))]
  transfers between devices with their start and end apart: 128 -> 0, of which waited for: 49 -> 0; matrix products, arithmetic and copies ran while one was open for 46% -> 0% of each run, Pallas kernels for 0% -> 0%
where the time goes in v1:
time: 86 us; the launch traced here: 84.4 us
  Pallas kernels  79.1 us (92%)
  local copies, waits for them, and re-layouts  5.28 us (6%)
    pallas_call x1, Pallas kernels, finish(): pl.pallas_call(finish_kernel, out_shape=jax.ShapeDtypeStruct((rows, width...  38.4 us
    pallas_call x1, Pallas kernels, attend(): pl.pallas_call(attend_kernel, out_shape=(jax.ShapeDtypeStruct((BLOCKS, TI...  20.8 us
    pallas_call x1, Pallas kernels, prepare(): pl.pallas_call(prepare_kernel, out_shape=(jax.ShapeDtypeStruct((Y, Z, C,...  19.8 us
    unnamed x12, local copies, waits for them, and re-layouts  5.28 us

profile of v1, /device:TPU:33, one launch (start us, length us, event | category | flops | bytes accessed | tf_op | source)
XLA Modules:
  0.0 84.4 jit_solution(15229470833105959566)
XLA Ops:
  0.0 1.0 %copy.6.table_ref = s32[512,64]{1,0:T(8,128)S(1)} copy(s32[512,64]{0,1:T(8,128)} %param.7) | data formatting | bytes 262144 | tf_op args[2]
  1.0 0.0 copy-start
  1.0 2.2 %copy-done = bf16[2,64,1,128,128]{4,3,2,1,0:T(8,128)(2,1)S(1)} copy-done((bf16[2,64,1,128,128]{4,3,2,1,0:T(8,128)(2,1)S(1)}, bf16[2,64,1,128,128]{4,3,2,1,0:T(8,128)(2,1)}, u32[]{:S(2)}) %copy-start) | copy-done | bytes 4194328
  3.2 0.0 copy-start.3
  3.2 0.8 copy-done.3
  4.0 0.0 copy-start.4
  4.0 0.7 copy-done.4
  4.7 0.0 copy-start.1
  4.7 19.8 %prepare.1 = (bf16[4,4,2,128,128]{4,3,2,1,0:T(8,128)(2,1)S(1)}, s32[8,512]{1,0:T(8,128)S(1)}, bf16[64,128,128]{2,1,0:T(8,128)(2,1)S(1)}) custom-call(bf16[128,128]{1,0:T(8,128)(2,1)S(1)} %bitcast.10, s32[512,64]{1,0:T(8,128)S(1)} %copy.6.table_ref, s32[1,512]{1,0:T(1,128)S(1)} %bitcast.12, bf16[2,64,128,128]{3,2,1,0:T(8,128)(2,1)S(1)} %bitcast.6), custom_call_target="tpu_custom_call" | custom-call | tf_op jit(solution)/shard_map/prepare/pallas_call | solution.py:188
  24.5 0.0 copy-start.2
  24.5 0.0 copy-done.1
  24.5 20.8 %attend.1 = (bf16[32,128,128]{2,1,0:T(8,128)(2,1)S(1)}, f32[32,2,128]{2,1,0:T(2,128)S(1)}) custom-call(s32[8,512]{1,0:T(8,128)S(1)} %get-tuple-element.10.pick, bf16[32,128,128]{2,1,0:T(8,128)(2,1)S(1)} %bitcast.8, bf16[64,128,128]{2,1,0:T(8,128)(2,1)S(1)} %get-tuple-element.12.kt_in, bf16[2,64,128,128]{3,2,1,0:T(8,128)(2,1)S(1)} %bitcast.7), custom_call_target="tpu_custom_call" | custom-call | tf_op jit(solution)/shard_map/attend/pallas_call | solution.py:320
  45.4 0.0 copy-done.2
  45.4 38.4 %finish.1 = bf16[64,256]{1,0:T(8,128)(2,1)S(1)} custom-call(bf16[4,4,2,128,128]{4,3,2,1,0:T(8,128)(2,1)S(1)} %bitcast.9, f32[4,4,2,2,128]{4,3,2,1,0:T(2,128)S(1)} %bitcast.11, bf16[1024,256]{1,0:T(8,128)(2,1)S(1)} %copy-done.2), custom_call_target="tpu_custom_call" | custom-call | tf_op jit(solution)/shard_map/finish/pallas_call | solution.py:448
  83.8 0.6 copy.8
Async XLA Ops:
  1.0 2.2 %copy-start = (bf16[2,64,1,128,128]{4,3,2,1,0:T(8,128)(2,1)S(1)}, bf16[2,64,1,128,128]{4,3,2,1,0:T(8,128)(2,1)}, u32[]{:S(2)}) copy-start(bf16[2,64,1,128,128]{4,3,2,1,0:T(8,128)(2,1)} %param.6) | copy-start | bytes 12582916
  3.2 0.8 copy-start.3
  4.0 0.7 copy-start.4
  4.7 19.9 %copy-start.1 = (bf16[2,64,1,128,128]{4,3,2,1,0:T(8,128)(2,1)S(1)}, bf16[2,64,1,128,128]{4,3,2,1,0:T(8,128)(2,1)}, u32[]{:S(2)}) copy-start(bf16[2,64,1,128,128]{4,3,2,1,0:T(8,128)(2,1)} %param.6) | copy-start | bytes 12582916
  24.5 20.9 %copy-start.2 = (bf16[1024,256]{1,0:T(8,128)(2,1)S(1)}, bf16[1024,256]{1,0:T(8,128)(2,1)}, u32[]{:S(2)}) copy-start(bf16[1024,256]{1,0:T(8,128)(2,1)} %w_ref.1) | copy-start | bytes 1572868

commit v2 on v1

v2 whole, which is shorter than its diff:
```python
import functools
import math

import jax
import jax.numpy as jnp
from jax import lax
from jax.experimental import pallas as pl
from jax.experimental.pallas import tpu as pltpu
from jax.sharding import PartitionSpec as P

Y, Z, C = 4, 4, 2
BLOCKS = Y * Z * C
ROWS = 16
HEADS = 8
HD = 128
PAGE = 128
PAGES = 64
SLOTS = 64
BATCH = BLOCKS * ROWS
TILE = ROWS * HEADS
GROUPS = 8
CAP = 4
CHUNK = 8
UNROLL = 8
NONE = 2560
STEPS = NONE // CHUNK // UNROLL
LOWEST = -1000.0
LOG2E_SCALE = math.log2(math.e) / math.sqrt(HD)
F32, BF16 = jnp.float32, jnp.bfloat16
VMEM = pltpu.VMEM


def position():
    me = lax.axis_index("seq")
    return me // (Z * C), (me // C) % Z, me % C


def at_seq(y, z, c):
    return {"seq": (y * Z + z) * C + c}


def send(src, dst, send_sem, recv_sem, device):
    copy = pltpu.make_async_remote_copy(
        src_ref=src, dst_ref=dst, send_sem=send_sem, recv_sem=recv_sem,
        device_id=device, device_id_type=pl.DeviceIdType.MESH,
    )
    copy.start()
    return copy


def arrived(dst, send_sem, recv_sem, device):
    pltpu.make_async_remote_copy(
        src_ref=dst, dst_ref=dst, send_sem=send_sem, recv_sem=recv_sem,
        device_id=device, device_id_type=pl.DeviceIdType.MESH,
    ).wait_recv()


def seq_peers(y, z, c):
    peers = [at_seq(y, z, 1 - c)]
    peers += [at_seq(y, (z + d) % Z, c) for d in range(1, Z)]
    peers += [at_seq((y + d) % Y, z, c) for d in range(1, Y)]
    return peers


def greet(peers):
    barrier = pltpu.get_barrier_semaphore()
    for peer in peers:
        pl.semaphore_signal(barrier, inc=1, device_id=peer, device_id_type=pl.DeviceIdType.MESH)
    pl.semaphore_wait(barrier, len(peers))


class Gather:
    def __init__(self, buf, zs, zr, ys, yr, ds, dr):
        self.buf, self.sems = buf, (zs, zr, ys, yr, ds, dr)
        self.y, self.z, self.c = position()
        self.copies = []

    def spread(self, dz):
        y, z, c = self.y, self.z, self.c
        zs, zr, ys, yr, ds, dr = self.sems
        block = self.buf.at[y, (z - dz + Z) % Z, c]
        for dy in (2, 1, 3):
            self.copies.append(send(block, block, ys.at[dy, dz], yr.at[dy, dz], at_seq((y + dy) % Y, z, c)))
        self.copies.append(send(block, block, ds.at[0, dz], dr.at[0, dz], at_seq(y, z, 1 - c)))

    def start(self):
        y, z, c = self.y, self.z, self.c
        zs, zr, ys, yr, ds, dr = self.sems
        own = self.buf.at[y, z, c]
        for dz in (2, 1, 3):
            self.copies.append(send(own, own, zs.at[dz], zr.at[dz], at_seq(y, (z + dz) % Z, c)))
        self.spread(0)

    def from_z(self, dz):
        y, z, c = self.y, self.z, self.c
        zs, zr, ys, yr, ds, dr = self.sems
        arrived(self.buf.at[y, (z - dz + Z) % Z, c], zs.at[dz], zr.at[dz], at_seq(y, (z - dz + Z) % Z, c))
        self.spread(dz)

    def from_y(self, dy, dz):
        y, z, c = self.y, self.z, self.c
        zs, zr, ys, yr, ds, dr = self.sems
        block = self.buf.at[(y - dy + Y) % Y, (z - dz + Z) % Z, c]
        arrived(block, ys.at[dy, dz], yr.at[dy, dz], at_seq((y - dy + Y) % Y, z, c))
        self.copies.append(send(block, block, ds.at[dy, dz], dr.at[dy, dz], at_seq(y, z, 1 - c)))

    def from_core(self, dy, dz):
        y, z, c = self.y, self.z, self.c
        zs, zr, ys, yr, ds, dr = self.sems
        block = self.buf.at[(y - dy + Y) % Y, (z - dz + Z) % Z, 1 - c]
        arrived(block, ds.at[dy, dz], dr.at[dy, dz], at_seq(y, z, 1 - c))

    def finish(self):
        for copy in self.copies:
            copy.wait_send()


ORDER = [(0, 0)] + [(0, d) for d in (1, 3, 2)] + [(dy, dz) for dz in (0, 1, 3, 2) for dy in (1, 3, 2)]
GATHER_SEMS = [
    pltpu.SemaphoreType.DMA((Z,)), pltpu.SemaphoreType.DMA((Z,)),
    pltpu.SemaphoreType.DMA((Y, Z)), pltpu.SemaphoreType.DMA((Y, Z)),
    pltpu.SemaphoreType.DMA((Y, Z)), pltpu.SemaphoreType.DMA((Y, Z)),
]


def dot(a, b, dims=((1,), (0,))):
    return lax.dot_general(a, b, (dims, ((), ())), preferred_element_type=F32)


def square(n, f):
    return f(lax.broadcasted_iota(jnp.int32, (n, n), 0), lax.broadcasted_iota(jnp.int32, (n, n), 1)).astype(F32).astype(BF16)


def selection(table, counts):
    own = lax.axis_index("seq")
    page = (table % PAGES).astype(F32)
    slot = lax.broadcasted_iota(jnp.int32, (SLOTS, BATCH), 0)
    present = (slot < counts) & (table // PAGES == own)
    rank = dot(square(SLOTS, jnp.greater_equal), present.astype(F32).astype(BF16))
    picks = [jnp.sum(jnp.where(present & (rank == k + 1.0), page + 1.0, 0.0), axis=0, keepdims=True) for k in range(CAP)]
    number = lax.broadcasted_iota(jnp.int32, (PAGES, BATCH), 0).astype(F32)
    takes = [number + 1.0 == pick for pick in picks]
    taken = sum(take.astype(F32) for take in takes)
    before = dot(taken.astype(BF16), square(BATCH, jnp.less_equal))
    chunks = jnp.floor((jnp.sum(taken, axis=1, keepdims=True) + (CHUNK - 1.0)) * (1.0 / CHUNK))
    first = dot(square(PAGES, jnp.greater), jnp.broadcast_to(chunks, (PAGES, 128)).astype(BF16))[:, 0:1]
    place = first * CHUNK + before - 1.0
    places = [
        jnp.where(pick > 0.0, jnp.sum(jnp.where(take, place, 0.0), axis=0, keepdims=True), float(NONE))
        for pick, take in zip(picks, takes)
    ]
    total = jnp.sum(chunks, axis=0, keepdims=True)
    group = lax.broadcasted_iota(jnp.int32, (BLOCKS, BATCH), 0)
    mine = group == lax.broadcasted_iota(jnp.int32, (BLOCKS, BATCH), 1) // ROWS
    column = lax.broadcasted_iota(jnp.int32, (BATCH, 128), 1)
    within = lax.broadcasted_iota(jnp.int32, (BATCH, 128), 0) % ROWS
    high = jnp.zeros((BLOCKS, 128), F32)
    low = jnp.zeros((BLOCKS, 128), F32)
    for k, p in enumerate(places):
        put = (column == k * ROWS + within).astype(F32).astype(BF16)
        upper = jnp.floor(p * (1.0 / 16.0))
        high += dot(jnp.where(mine, upper, 0.0).astype(BF16), put)
        low += dot(jnp.where(mine, p - upper * 16.0, 0.0).astype(BF16), put)
    lane = lax.broadcasted_iota(jnp.int32, (BLOCKS, 128), 1)
    pick = jnp.where(lane == CAP * ROWS, total, high * 16.0 + low)
    chunk = lax.broadcasted_iota(jnp.int32, (PAGES, BATCH), 1).astype(F32)
    page_of = jnp.sum(jnp.where((first <= chunk) & (chunk < first + chunks), number, 0.0), axis=0, keepdims=True)
    step = lax.broadcasted_iota(jnp.int32, (STEPS, BATCH), 0)
    its = step == lax.broadcasted_iota(jnp.int32, (STEPS, BATCH), 1) // UNROLL
    put = (column == 64 + lax.broadcasted_iota(jnp.int32, (BATCH, 128), 0) % UNROLL).astype(F32).astype(BF16)
    pages = dot(jnp.where(its, page_of, 0.0).astype(BF16), put)
    return places, pick.astype(jnp.int32), pages.astype(jnp.int32)


def owners(places, start):
    at = lax.broadcasted_iota(jnp.int32, (256, BATCH), 0).astype(F32) + start.astype(F32)
    hit = (at == places[0:1]) | (at == places[1:2]) | (at == places[2:3]) | (at == places[3:4])
    who = lax.broadcasted_iota(jnp.int32, (8, BATCH), 1)
    digit = jnp.where(lax.broadcasted_iota(jnp.int32, (8, BATCH), 0) == 0, who // 16, who % 16)
    digits = dot(digit.astype(F32).astype(BF16), jnp.where(hit, 1.0, 0.0).astype(BF16), ((1,), (1,)))
    return (digits[0:1] * 16.0 + digits[1:2]).astype(jnp.int32)


def prepare_kernel(
    q_ref, table_ref, counts_ref, cache_ref, all_ref, pick_ref, who_ref, kt_ref, v_ref,
    table, counts, keys, places, pages, in_sems, key_sems, *sems,
):
    y, z, c = position()
    half = PAGES // 2
    small = [
        pltpu.make_async_copy(q_ref, all_ref.at[y, z, c], in_sems.at[0]),
        pltpu.make_async_copy(table_ref, table, in_sems.at[1]),
        pltpu.make_async_copy(counts_ref, counts, in_sems.at[2]),
    ]
    loads = [
        pltpu.make_async_copy(cache_ref.at[0, pl.ds(i * half, half)], keys.at[pl.ds(i * half, half)], key_sems.at[i])
        for i in range(2)
    ]
    load_v = pltpu.make_async_copy(cache_ref.at[1], v_ref, in_sems.at[3])
    for load in small + loads:
        load.start()
    greet(seq_peers(y, z, c))
    small[0].wait()
    gather = Gather(all_ref, *sems)
    gather.start()
    load_v.start()
    small[1].wait()
    small[2].wait()
    rows, pick_ref[...], pages[...] = selection(table[...], counts[...])
    for k in range(CAP):
        places[k : k + 1] = rows[k]

    def turn(i, carry):
        for j in range(4):
            kt_ref[i * 4 + j] = keys[i * 4 + j].T
        return carry

    def name(i, carry):
        lane = lax.broadcasted_iota(jnp.int32, (1, 128), 1)
        who = owners(places, i * 256)
        for j in range(2):
            half_row = who[:, j * 128 : (j + 1) * 128]
            rolled = pltpu.roll(jnp.broadcast_to(half_row, (8, 128)), 64, 1)[0:1]
            row = 4 * i + 2 * j
            who_ref[pl.ds(row, 1)] = jnp.where(lane < 64, half_row, pages[pl.ds(row, 1)])
            who_ref[pl.ds(row + 1, 1)] = jnp.where(lane < 64, rolled, pages[pl.ds(row + 1, 1)])
        return carry

    loads[0].wait()
    lax.fori_loop(0, 8, turn, 0)
    for dz in (1, 3, 2):
        gather.from_z(dz)
    loads[1].wait()
    lax.fori_loop(8, 16, turn, 0)
    lax.fori_loop(0, NONE // 256, name, 0)
    for dy, dz in ORDER[4:]:
        gather.from_y(dy, dz)
    for dy, dz in ORDER:
        gather.from_core(dy, dz)
    gather.finish()
    load_v.wait()


def prepare(q, table, counts, cache):
    vmem = pl.BlockSpec(memory_space=VMEM)
    hbm = pl.BlockSpec(memory_space=pltpu.HBM)
    return pl.pallas_call(
        prepare_kernel,
        out_shape=(
            jax.ShapeDtypeStruct((Y, Z, C, TILE, HD), BF16),
            jax.ShapeDtypeStruct((BLOCKS, 128), jnp.int32),
            jax.ShapeDtypeStruct((STEPS, 128), jnp.int32),
            jax.ShapeDtypeStruct((PAGES, HD, PAGE), BF16),
            jax.ShapeDtypeStruct((PAGES, PAGE, HD), BF16),
        ),
        in_specs=[hbm, hbm, hbm, hbm],
        out_specs=(vmem,) * 5,
        scratch_shapes=[
            VMEM((SLOTS, BATCH), jnp.int32),
            VMEM((1, BATCH), jnp.int32),
            VMEM((PAGES, PAGE, HD), BF16),
            VMEM((8, BATCH), F32),
            VMEM((STEPS, 128), jnp.int32),
            pltpu.SemaphoreType.DMA((4,)),
            pltpu.SemaphoreType.DMA((2,)),
            *GATHER_SEMS,
        ],
        compiler_params=pltpu.CompilerParams(collective_id=0, has_side_effects=True, vmem_limit_bytes=24 << 20),
        name="prepare",
    )(q, table, counts, cache)


def attend_kernel(pick, who, q_in, kt, v, acc_out, stats_out, q, scores, found):
    def widen(i, carry):
        for j in range(4):
            q[pl.ds((i * 4 + j) * ROWS, ROWS)] = q_in[i * 4 + j].astype(F32).reshape(ROWS, HEADS, HD)
        return carry

    lax.fori_loop(0, BLOCKS // 4, widen, 0)
    found[pl.ds(NONE, 8), 0] = jnp.zeros((8, HEADS, HD), F32)
    found[pl.ds(NONE, 8), 1] = jnp.full((8, HEADS, HD), -1e30, F32)
    ones = jnp.ones((PAGE, HD), BF16)

    def scores_of(g):
        for u in range(UNROLL):
            left = jnp.concatenate([q[who[g, u * CHUNK + j]] for j in range(CHUNK)], axis=0).astype(BF16)
            scores[u] = dot(left, kt[who[g, 64 + u]])

    def weigh(g):
        for u in range(UNROLL):
            at = pl.ds((g * UNROLL + u) * CHUNK, CHUNK)
            s = scores[u] * LOG2E_SCALE
            m = jnp.max(s, axis=1, keepdims=True)
            w = jnp.exp2(s - m).astype(BF16)
            o = dot(w, jnp.concatenate([v[who[g, 64 + u]], ones], axis=1))
            total = o[:, HD:]
            found[at, 0] = (o[:, :HD] / total).reshape(CHUNK, HEADS, HD)
            found[at, 1] = (m + jnp.log2(total)).reshape(CHUNK, HEADS, HD)

    scores_of(0)
    steps = (pick[0, CAP * ROWS] + UNROLL - 1) // UNROLL

    def step(g, carry):
        weigh(g)
        scores_of(jnp.minimum(g + 1, STEPS - 1))
        return carry

    lax.fori_loop(0, steps, step, 0)
    sublane = lax.broadcasted_iota(jnp.int32, (HEADS, HD), 0)
    lane = lax.broadcasted_iota(jnp.int32, (HEADS, HD), 1)

    def close(g, carry):
        tops = jnp.zeros((HEADS, HD), F32)
        totals = jnp.zeros((HEADS, HD), F32)
        outs = []
        for s in range(ROWS):
            at = [pick[g, k * ROWS + s] for k in range(CAP)]
            weights = [found[p, 1] for p in at]
            highest = functools.reduce(jnp.maximum, weights)
            m = jnp.maximum(jnp.floor(highest * 0.5 + 0.5) * 2.0, LOWEST)
            factors = [jnp.exp2(w - m) for w in weights]
            outs.append(sum(f * found[p, 0] for f, p in zip(factors, at)))
            here = lane - sublane == s * HEADS
            tops = jnp.where(here, m, tops)
            totals = jnp.where(here, sum(factors), totals)
        stats_out[g, 0:1] = jnp.sum(tops, axis=0, keepdims=True)
        stats_out[g, 1:2] = jnp.sum(totals, axis=0, keepdims=True)
        acc_out[g] = jnp.concatenate(outs, axis=0).astype(BF16)
        return carry

    lax.fori_loop(0, BLOCKS, close, 0)


def attend(pick, who, q, kt, v):
    vmem = pl.BlockSpec(memory_space=VMEM)
    smem = pl.BlockSpec(memory_space=pltpu.SMEM)
    return pl.pallas_call(
        attend_kernel,
        out_shape=(
            jax.ShapeDtypeStruct((BLOCKS, TILE, HD), BF16),
            jax.ShapeDtypeStruct((BLOCKS, 2, HD), F32),
        ),
        in_specs=[smem, smem, vmem, vmem, vmem],
        out_specs=(vmem, vmem),
        scratch_shapes=[
            VMEM((BATCH, HEADS, HD), F32),
            VMEM((UNROLL, CHUNK * HEADS, PAGE), F32),
            VMEM((NONE + 8, 2, HEADS, HD), F32),
        ],
        compiler_params=pltpu.CompilerParams(vmem_limit_bytes=40 << 20),
        name="attend",
    )(pick, who, q, kt, v)


def merge(parts, stats, diagonal):
    m = functools.reduce(jnp.maximum, [s[0:1] for s in stats])
    factors = [jnp.exp2(s[0:1] - m) for s in stats]
    total = sum(s[1:2] * f for s, f in zip(stats, factors))
    left = jnp.concatenate([jnp.where(diagonal, jnp.broadcast_to(f, (TILE, TILE)), 0.0).astype(BF16) for f in factors], axis=1)
    return dot(left, jnp.concatenate(parts, axis=0)), m, total


def finish_kernel(
    acc, stats, w_ref, out_ref,
    core_acc, core_stats, y_out, y_out_stats, y_in, y_in_stats, z_out, z_out_stats, z_in, z_in_stats,
    turned, att, w, part, parts_in, w_sem,
    c_send, c_recv, cs_send, cs_recv, y_send, y_recv, ys_send, ys_recv, z_send, z_recv, zs_send, zs_recv, h_send, h_recv, *sems,
):
    y, z, c = position()
    h = lax.axis_index("head")
    other = 1 - c
    load_w = pltpu.make_async_copy(w_ref, w, w_sem)
    load_w.start()
    greet(seq_peers(y, z, c) + [{"head": (h + d) % GROUPS} for d in range(1, GROUPS)])
    copies = []
    partner = at_seq(y, z, other)
    order = (2, 1, 3, 0)
    for e in order:
        zz = (z + e) % Z
        copies.append(send(acc.at[:, zz, other], core_acc.at[e], c_send.at[e], c_recv.at[e], partner))
        copies.append(send(stats.at[:, zz, other], core_stats.at[e], cs_send.at[e], cs_recv.at[e], partner))
    diagonal = lax.broadcasted_iota(jnp.int32, (TILE, TILE), 0) == lax.broadcasted_iota(jnp.int32, (TILE, TILE), 1)

    def put(values, rows, o, m, total):
        values[...] = o.astype(BF16)
        rows[0:1] = m
        rows[1:2] = total

    for e in order:
        zz = (z + e) % Z
        arrived(core_acc.at[e], c_send.at[e], c_recv.at[e], partner)
        arrived(core_stats.at[e], cs_send.at[e], cs_recv.at[e], partner)
        for d in order:
            yy = (y + d) % Y
            merged = merge([acc[yy, zz, c], core_acc[e, yy]], [stats[yy, zz, c], core_stats[e, yy]], diagonal)
            if d == 0:
                put(y_in.at[0, e], y_in_stats.at[0, e], *merged)
            else:
                put(y_out.at[d, e], y_out_stats.at[d, e], *merged)
                there = at_seq(yy, z, c)
                copies.append(send(y_out.at[d, e], y_in.at[d, e], y_send.at[d, e], y_recv.at[d, e], there))
                copies.append(send(y_out_stats.at[d, e], y_in_stats.at[d, e], ys_send.at[d, e], ys_recv.at[d, e], there))
    for e in order:
        for d in (1, 3, 2):
            there = at_seq((y - d + Y) % Y, z, c)
            arrived(y_in.at[d, e], y_send.at[d, e], y_recv.at[d, e], there)
            arrived(y_in_stats.at[d, e], ys_send.at[d, e], ys_recv.at[d, e], there)
        merged = merge([y_in[d, e] for d in range(Y)], [y_in_stats[d, e] for d in range(Y)], diagonal)
        if e == 0:
            put(z_in.at[0], z_in_stats.at[0], *merged)
        else:
            put(z_out.at[e], z_out_stats.at[e], *merged)
            there = at_seq(y, (z + e) % Z, c)
            copies.append(send(z_out.at[e], z_in.at[e], z_send.at[e], z_recv.at[e], there))
            copies.append(send(z_out_stats.at[e], z_in_stats.at[e], zs_send.at[e], zs_recv.at[e], there))
    for e in (2, 1, 3):
        there = at_seq(y, (z - e + Z) % Z, c)
        arrived(z_in.at[e], z_send.at[e], z_recv.at[e], there)
        arrived(z_in_stats.at[e], zs_send.at[e], zs_recv.at[e], there)
    o, m, total = merge([z_in[e] for e in range(Z)], [z_in_stats[e] for e in range(Z)], diagonal)
    turned[...] = o / jnp.broadcast_to(total, (TILE, TILE)).T
    for i in range(HEADS):
        att[y, z, c, :, i * HD : (i + 1) * HD] = turned[pl.ds(i, ROWS, stride=HEADS), :].astype(BF16)
    gather = Gather(att, *sems)
    gather.start()
    near = 3 - 2 * (z % 2)
    far = Z - near
    gather.from_z(near)
    gather.from_z(far)
    gather.from_y(1, 0)
    gather.from_y(3, 0)
    gather.from_z(2)
    gather.from_y(2, 0)
    for dy in (1, 3, 2):
        gather.from_y(dy, near)
    load_w.wait()

    def project(pair):
        for yy in range(Y):
            to = yy * 2 + pair
            rows = jnp.concatenate([att[yy, pair * 2 + i, j] for i in range(2) for j in range(C)], axis=0)
            share = dot(rows, w[...]).astype(BF16)

            @pl.when(to == h)
            def _():
                parts_in[h] = share

            @pl.when(to != h)
            def _():
                part[to] = share
                send(part.at[to], parts_in.at[h], h_send.at[to], h_recv.at[h], {"head": to})

    for dz in (0, near):
        for dy in (0, 1, 3, 2):
            gather.from_core(dy, dz)
    project(z // 2)
    for dz in (far, 2):
        for dy in (1, 3, 2):
            gather.from_y(dy, dz)
    for dz in (far, 2):
        for dy in (0, 1, 3, 2):
            gather.from_core(dy, dz)
    project(1 - z // 2)
    for s in range(GROUPS):

        @pl.when(s != h)
        def _():
            arrived(parts_in.at[s], h_send.at[s], h_recv.at[s], {"head": s})

    out_ref[...] = sum(parts_in[s].astype(F32) for s in range(GROUPS)).astype(BF16)
    for s in range(GROUPS):

        @pl.when(s != h)
        def _():
            pltpu.make_async_remote_copy(
                src_ref=part.at[s], dst_ref=parts_in.at[h], send_sem=h_send.at[s], recv_sem=h_recv.at[h],
                device_id={"head": s}, device_id_type=pl.DeviceIdType.MESH,
            ).wait_send()

    gather.finish()
    for copy in copies:
        copy.wait_send()


def finish(acc, stats, w):
    vmem = pl.BlockSpec(memory_space=VMEM)
    width = w.shape[1]
    rows = BATCH // GROUPS
    dma = pltpu.SemaphoreType.DMA
    return pl.pallas_call(
        finish_kernel,
        out_shape=jax.ShapeDtypeStruct((rows, width), BF16),
        in_specs=[vmem, vmem, pl.BlockSpec(memory_space=pltpu.HBM)],
        out_specs=vmem,
        scratch_shapes=[
            VMEM((Z, Y, TILE, HD), BF16), VMEM((Z, Y, 2, HD), F32),
            VMEM((Y, Z, TILE, HD), BF16), VMEM((Y, Z, 2, HD), F32),
            VMEM((Y, Z, TILE, HD), BF16), VMEM((Y, Z, 2, HD), F32),
            VMEM((Z, TILE, HD), BF16), VMEM((Z, 2, HD), F32),
            VMEM((Z, TILE, HD), BF16), VMEM((Z, 2, HD), F32),
            VMEM((TILE, HD), F32),
            VMEM((Y, Z, C, ROWS, HEADS * HD), BF16),
            VMEM((HEADS * HD, width), BF16),
            VMEM((GROUPS, rows, width), BF16), VMEM((GROUPS, rows, width), BF16),
            dma,
            *[dma((Z,)) for _ in range(4)],
            *[dma((Y, Z)) for _ in range(4)],
            *[dma((Z,)) for _ in range(4)],
            dma((GROUPS,)), dma((GROUPS,)),
            *GATHER_SEMS,
        ],
        compiler_params=pltpu.CompilerParams(collective_id=1, has_side_effects=True, vmem_limit_bytes=32 << 20),
        name="finish",
    )(acc, stats, w)


def shards(queries, cache, page_table, page_count, out_weight):
    cache = cache.reshape(2, PAGES, PAGE, HD)
    stay = functools.partial(pltpu.with_memory_space_constraint, memory_space=pltpu.HBM)
    q, pick, who, kt, v = prepare(stay(queries.reshape(TILE, HD)), stay(page_table.T), stay(page_count.reshape(1, BATCH)), stay(cache))
    acc, stats = attend(pick, who, q.reshape(BLOCKS, TILE, HD), kt, v)
    return finish(acc.reshape(Y, Z, C, TILE, HD), stats.reshape(Y, Z, C, 2, HD), stay(out_weight))


def solution(mesh):
    return jax.shard_map(
        shards,
        mesh=mesh,
        in_specs=(
            P("seq", "head", None),
            P(None, "seq", "head", None, None),
            P(),
            P(),
            P("head", "seq"),
        ),
        out_specs=P("head", "seq"),
        check_vma=False,
    )
```

time: 86 us -> 66.6 us (0.77)
  Pallas kernels: 79.1 us -> 65 us
  local copies, waits for them, and re-layouts: 5.28 us -> 0.62 us
    pallas_call x1, Pallas kernels: 20.8 us -> 10.3 us  [attend(): pl.pallas_call(attend_kernel, out_shape=(jax.ShapeDtypeStruct((BLOCKS, TI...]
    unnamed x12 -> x1, local copies, waits for them, and re-layouts: 5.28 us -> 0.62 us
    pallas_call x1, Pallas kernels: 38.4 us -> 35 us  [finish(): pl.pallas_call(finish_kernel, out_shape=jax.ShapeDtypeStruct((rows, width...]
where the time goes in v2:
time: 66.6 us; the launch traced here: 65.7 us
  Pallas kernels  65 us (98%)
    pallas_call x1, Pallas kernels, finish(): pl.pallas_call(finish_kernel, out_shape=jax.ShapeDtypeStruct((rows, width...  35 us
    pallas_call x1, Pallas kernels, prepare(): pl.pallas_call(prepare_kernel, out_shape=(jax.ShapeDtypeStruct((Y, Z, C,...  19.8 us
    pallas_call x1, Pallas kernels, attend(): pl.pallas_call(attend_kernel, out_shape=(jax.ShapeDtypeStruct((BLOCKS, TI...  10.3 us

profile of v2, /device:TPU:33, one launch (start us, length us, event | category | flops | bytes accessed | tf_op | source)
XLA Modules:
  0.0 65.7 jit_solution(14939343387676103911)
XLA Ops:
  0.0 19.8 %prepare.1 = (bf16[4,4,2,128,128]{4,3,2,1,0:T(8,128)(2,1)S(1)}, s32[32,128]{1,0:T(8,128)S(1)}, s32[40,128]{1,0:T(8,128)S(1)}, bf16[64,128,128]{2,1,0:T(8,128)(2,1)S(1)}, bf16[64,128,128]{2,1,0:T(8,128)(2,1)S(1)}) custom-call(bf16[128,128]{1,0:T(8,128)(2,1)} %bitcast.12, s32[64,512]{1,0:T(8,128)} %bitcast.11, s32[1,512]{1,0:T(1,128)} %bitcast.13, ...), custom_call_target="tpu_custom_call" | custom-call | tf_op jit(solution)/shard_map/prepare/pallas_call | solution.py:247
  19.8 10.3 %attend.1 = (bf16[32,128,128]{2,1,0:T(8,128)(2,1)S(1)}, f32[32,2,128]{2,1,0:T(2,128)S(1)}) custom-call(s32[32,128]{1,0:T(8,128)S(1)} %get-tuple-element.12.pick, s32[40,128]{1,0:T(8,128)S(1)} %get-tuple-element.13.who, bf16[32,128,128]{2,1,0:T(8,128)(2,1)S(1)} %bitcast.8, bf16[64,128,128]{2,1,0:T(8,128)(2,1)S(1)} %get-tuple-element.15.kt, ...), custom_call_target="tpu_custom_call" | custom-call | tf_op jit(solution)/shard_map/attend/pallas_call | solution.py:337
  30.1 35.0 %finish.1 = bf16[64,256]{1,0:T(8,128)(2,1)S(1)} custom-call(bf16[4,4,2,128,128]{4,3,2,1,0:T(8,128)(2,1)S(1)} %bitcast.7, f32[4,4,2,2,128]{4,3,2,1,0:T(2,128)S(1)} %bitcast.9, bf16[1024,256]{1,0:T(8,128)(2,1)} %w_ref.1), custom_call_target="tpu_custom_call" | custom-call | tf_op jit(solution)/shard_map/finish/pallas_call | solution.py:490
  65.0 0.6 copy.7

commit v3 on v2

--- a/solution.py
+++ b/solution.py
@@ -62,10 +62,12 @@
     return peers
 
 
-def greet(peers):
+def greet(peers, meanwhile=None):
     barrier = pltpu.get_barrier_semaphore()
     for peer in peers:
         pl.semaphore_signal(barrier, inc=1, device_id=peer, device_id_type=pl.DeviceIdType.MESH)
+    if meanwhile is not None:
+        meanwhile()
     pl.semaphore_wait(barrier, len(peers))
 
 
@@ -265,12 +267,12 @@
             pltpu.SemaphoreType.DMA((2,)),
             *GATHER_SEMS,
         ],
-        compiler_params=pltpu.CompilerParams(collective_id=0, has_side_effects=True, vmem_limit_bytes=24 << 20),
+        compiler_params=pltpu.CompilerParams(collective_id=0, has_side_effects=True, vmem_limit_bytes=12 << 20),
         name="prepare",
     )(q, table, counts, cache)
 
 
-def attend_kernel(pick, who, q_in, kt, v, acc_out, stats_out, q, scores, found):
+def attend_kernel(pick, who, q_in, kt, v, found, q, scores):
     def widen(i, carry):
         for j in range(4):
             q[pl.ds((i * 4 + j) * ROWS, ROWS)] = q_in[i * 4 + j].astype(F32).reshape(ROWS, HEADS, HD)
@@ -306,29 +308,6 @@
         return carry
 
     lax.fori_loop(0, steps, step, 0)
-    sublane = lax.broadcasted_iota(jnp.int32, (HEADS, HD), 0)
-    lane = lax.broadcasted_iota(jnp.int32, (HEADS, HD), 1)
-
-    def close(g, carry):
-        tops = jnp.zeros((HEADS, HD), F32)
-        totals = jnp.zeros((HEADS, HD), F32)
-        outs = []
-        for s in range(ROWS):
-            at = [pick[g, k * ROWS + s] for k in range(CAP)]
-            weights = [found[p, 1] for p in at]
-            highest = functools.reduce(jnp.maximum, weights)
-            m = jnp.maximum(jnp.floor(highest * 0.5 + 0.5) * 2.0, LOWEST)
-            factors = [jnp.exp2(w - m) for w in weights]
-            outs.append(sum(f * found[p, 0] for f, p in zip(factors, at)))
-            here = lane - sublane == s * HEADS
-            tops = jnp.where(here, m, tops)
-            totals = jnp.where(here, sum(factors), totals)
-        stats_out[g, 0:1] = jnp.sum(tops, axis=0, keepdims=True)
-        stats_out[g, 1:2] = jnp.sum(totals, axis=0, keepdims=True)
-        acc_out[g] = jnp.concatenate(outs, axis=0).astype(BF16)
-        return carry
-
-    lax.fori_loop(0, BLOCKS, close, 0)
 
 
 def attend(pick, who, q, kt, v):
@@ -336,20 +315,36 @@
     smem = pl.BlockSpec(memory_space=pltpu.SMEM)
     return pl.pallas_call(
         attend_kernel,
-        out_shape=(
-            jax.ShapeDtypeStruct((BLOCKS, TILE, HD), BF16),
-            jax.ShapeDtypeStruct((BLOCKS, 2, HD), F32),
-        ),
+        out_shape=VMEM((NONE + 8, 2, HEADS, HD), F32),
         in_specs=[smem, smem, vmem, vmem, vmem],
-        out_specs=(vmem, vmem),
+        out_specs=vmem,
         scratch_shapes=[
             VMEM((BATCH, HEADS, HD), F32),
             VMEM((UNROLL, CHUNK * HEADS, PAGE), F32),
-            VMEM((NONE + 8, 2, HEADS, HD), F32),
         ],
-        compiler_params=pltpu.CompilerParams(vmem_limit_bytes=40 << 20),
+        compiler_params=pltpu.CompilerParams(vmem_limit_bytes=8 << 20),
         name="attend",
     )(pick, who, q, kt, v)
+
+
+def settle(pick, found, g, values, stats):
+    sublane = lax.broadcasted_iota(jnp.int32, (HEADS, HD), 0)
+    lane = lax.broadcasted_iota(jnp.int32, (HEADS, HD), 1)
+    tops = jnp.zeros((HEADS, HD), F32)
+    totals = jnp.zeros((HEADS, HD), F32)
+    outs = []
+    for s in range(ROWS):
+        at = [pick[g, k * ROWS + s] for k in range(CAP)]
+        highest = [found[p, 1] for p in at]
+        m = jnp.maximum(jnp.floor(functools.reduce(jnp.maximum, highest) * 0.5 + 0.5) * 2.0, LOWEST)
+        factors = [jnp.exp2(t - m) for t in highest]
+        outs.append(sum(f * found[p, 0] for f, p in zip(factors, at)))
+        here = lane - sublane == s * HEADS
+        tops = jnp.where(here, m, tops)
+        totals = jnp.where(here, sum(factors), totals)
+    stats[0:1] = jnp.sum(tops, axis=0, keepdims=True)
+    stats[1:2] = jnp.sum(totals, axis=0, keepdims=True)
+    values[...] = jnp.concatenate(outs, axis=0).astype(BF16)
 
 
 def merge(parts, stats, diagonal):
@@ -361,7 +356,8 @@
 
 
 def finish_kernel(
-    acc, stats, w_ref, out_ref,
+    pick, found, w_ref, out_ref,
+    own_acc, own_stats, their_acc, their_stats,
     core_acc, core_stats, y_out, y_out_stats, y_in, y_in_stats, z_out, z_out_stats, z_in, z_in_stats,
     turned, att, w, part, parts_in, w_sem,
     c_send, c_recv, cs_send, cs_recv, y_send, y_recv, ys_send, ys_recv, z_send, z_recv, zs_send, zs_recv, h_send, h_recv, *sems,
@@ -371,14 +367,25 @@
     other = 1 - c
     load_w = pltpu.make_async_copy(w_ref, w, w_sem)
     load_w.start()
-    greet(seq_peers(y, z, c) + [{"head": (h + d) % GROUPS} for d in range(1, GROUPS)])
-    copies = []
     partner = at_seq(y, z, other)
     order = (2, 1, 3, 0)
+
+    def settle_all(e, core, values, stats):
+        def one(yy, carry):
+            settle(pick, found, (yy * Z + (z + e) % Z) * C + core, values.at[e, yy], stats.at[e, yy])
+            return carry
+
+        lax.fori_loop(0, Y, one, 0)
+
+    def theirs():
+        for e in order:
+            settle_all(e, other, their_acc, their_stats)
+
+    greet(seq_peers(y, z, c) + [{"head": (h + d) % GROUPS} for d in range(1, GROUPS)], theirs)
+    copies = []
     for e in order:
-        zz = (z + e) % Z
-        copies.append(send(acc.at[:, zz, other], core_acc.at[e], c_send.at[e], c_recv.at[e], partner))
-        copies.append(send(stats.at[:, zz, other], core_stats.at[e], cs_send.at[e], cs_recv.at[e], partner))
+        copies.append(send(their_acc.at[e], core_acc.at[e], c_send.at[e], c_recv.at[e], partner))
+        copies.append(send(their_stats.at[e], core_stats.at[e], cs_send.at[e], cs_recv.at[e], partner))
     diagonal = lax.broadcasted_iota(jnp.int32, (TILE, TILE), 0) == lax.broadcasted_iota(jnp.int32, (TILE, TILE), 1)
 
     def put(values, rows, o, m, total):
@@ -387,12 +394,12 @@
         rows[1:2] = total
 
     for e in order:
-        zz = (z + e) % Z
+        settle_all(e, c, own_acc, own_stats)
         arrived(core_acc.at[e], c_send.at[e], c_recv.at[e], partner)
         arrived(core_stats.at[e], cs_send.at[e], cs_recv.at[e], partner)
         for d in order:
             yy = (y + d) % Y
-            merged = merge([acc[yy, zz, c], core_acc[e, yy]], [stats[yy, zz, c], core_stats[e, yy]], diagonal)
+            merged = merge([own_acc[e, yy], core_acc[e, yy]], [own_stats[e, yy], core_stats[e, yy]], diagonal)
             if d == 0:
                 put(y_in.at[0, e], y_in_stats.at[0, e], *merged)
             else:
@@ -482,7 +489,7 @@
         copy.wait_send()
 
 
-def finish(acc, stats, w):
+def finish(pick, found, w):
     vmem = pl.BlockSpec(memory_space=VMEM)
     width = w.shape[1]
     rows = BATCH // GROUPS
@@ -490,9 +497,11 @@
     return pl.pallas_call(
         finish_kernel,
         out_shape=jax.ShapeDtypeStruct((rows, width), BF16),
-        in_specs=[vmem, vmem, pl.BlockSpec(memory_space=pltpu.HBM)],
+        in_specs=[pl.BlockSpec(memory_space=pltpu.SMEM), vmem, pl.BlockSpec(memory_space=pltpu.HBM)],
         out_specs=vmem,
         scratch_shapes=[
+            VMEM((Z, Y, TILE, HD), BF16), VMEM((Z, Y, 2, HD), F32),
+            VMEM((Z, Y, TILE, HD), BF16), VMEM((Z, Y, 2, HD), F32),
             VMEM((Z, Y, TILE, HD), BF16), VMEM((Z, Y, 2, HD), F32),
             VMEM((Y, Z, TILE, HD), BF16), VMEM((Y, Z, 2, HD), F32),
             VMEM((Y, Z, TILE, HD), BF16), VMEM((Y, Z, 2, HD), F32),
@@ -509,17 +518,17 @@
             dma((GROUPS,)), dma((GROUPS,)),
             *GATHER_SEMS,
         ],
-        compiler_params=pltpu.CompilerParams(collective_id=1, has_side_effects=True, vmem_limit_bytes=32 << 20),
+        compiler_params=pltpu.CompilerParams(collective_id=1, has_side_effects=True, vmem_limit_bytes=12 << 20),
         name="finish",
-    )(acc, stats, w)
+    )(pick, found, w)
 
 
 def shards(queries, cache, page_table, page_count, out_weight):
     cache = cache.reshape(2, PAGES, PAGE, HD)
     stay = functools.partial(pltpu.with_memory_space_constraint, memory_space=pltpu.HBM)
     q, pick, who, kt, v = prepare(stay(queries.reshape(TILE, HD)), stay(page_table.T), stay(page_count.reshape(1, BATCH)), stay(cache))
-    acc, stats = attend(pick, who, q.reshape(BLOCKS, TILE, HD), kt, v)
-    return finish(acc.reshape(Y, Z, C, TILE, HD), stats.reshape(Y, Z, C, 2, HD), stay(out_weight))
+    found = attend(pick, who, q.reshape(BLOCKS, TILE, HD), kt, v)
+    return finish(pick, found, stay(out_weight))
 
 
 def solution(mesh):

time: 66.6 us -> 64.6 us (0.970); the launches traced: 65.7 us -> 64.8 us
  Pallas kernels: 65 us -> 64.2 us
    pallas_call x1, Pallas kernels: 10.3 us -> 7.23 us  [attend(): pl.pallas_call(attend_kernel, out_shape=VMEM((NONE + 8, 2, HEADS, HD), F3...]
    pallas_call x1, Pallas kernels: 35 us -> 37.1 us  [finish(): pl.pallas_call(finish_kernel, out_shape=jax.ShapeDtypeStruct((rows, width...]
where the time goes in v3:
time: 64.6 us; the launch traced here: 64.8 us
  Pallas kernels  64.2 us (99%)
    pallas_call x1, Pallas kernels, finish(): pl.pallas_call(finish_kernel, out_shape=jax.ShapeDtypeStruct((rows, width...  37.1 us
    pallas_call x1, Pallas kernels, prepare(): pl.pallas_call(prepare_kernel, out_shape=(jax.ShapeDtypeStruct((Y, Z, C,...  19.8 us
    pallas_call x1, Pallas kernels, attend(): pl.pallas_call(attend_kernel, out_shape=VMEM((NONE + 8, 2, HEADS, HD), F3...  7.23 us

profile of v3, /device:TPU:33, one launch (start us, length us, event | category | flops | bytes accessed | tf_op | source)
XLA Modules:
  0.0 64.8 jit_solution(13711261847429028209)
XLA Ops:
  0.0 19.8 %prepare.1 = (bf16[4,4,2,128,128]{4,3,2,1,0:T(8,128)(2,1)S(1)}, s32[32,128]{1,0:T(8,128)S(1)}, s32[40,128]{1,0:T(8,128)S(1)}, bf16[64,128,128]{2,1,0:T(8,128)(2,1)S(1)}, bf16[64,128,128]{2,1,0:T(8,128)(2,1)S(1)}) custom-call(bf16[128,128]{1,0:T(8,128)(2,1)} %bitcast.8, s32[64,512]{1,0:T(8,128)} %bitcast.7, s32[1,512]{1,0:T(1,128)} %bitcast.9, ...), custom_call_target="tpu_custom_call" | custom-call | tf_op jit(solution)/shard_map/prepare/pallas_call | solution.py:249
  19.8 7.2 %attend.1.found = f32[2568,2,8,128]{3,2,1,0:T(8,128)S(1)} custom-call(s32[32,128]{1,0:T(8,128)S(1)} %get-tuple-element.10.pick, s32[40,128]{1,0:T(8,128)S(1)} %get-tuple-element.11.who, bf16[32,128,128]{2,1,0:T(8,128)(2,1)S(1)} %bitcast.5, bf16[64,128,128]{2,1,0:T(8,128)(2,1)S(1)} %get-tuple-element.13.kt, bf16[64,128,128]{2,1,0:T(8,128)(2,1)S(1)} %get-tuple-element.14.v), custom_call_target="tpu_custom_call" | custom-call | tf_op jit(solution)/shard_map/attend/pallas_call | solution.py:316
  27.0 37.1 %finish.1 = bf16[64,256]{1,0:T(8,128)(2,1)S(1)} custom-call(s32[32,128]{1,0:T(8,128)S(1)} %get-tuple-element.10.pick, f32[2568,2,8,128]{3,2,1,0:T(8,128)S(1)} %attend.1.found, bf16[1024,256]{1,0:T(8,128)(2,1)} %w_ref.1), custom_call_target="tpu_custom_call" | custom-call | tf_op jit(solution)/shard_map/finish/pallas_call | solution.py:497
  64.2 0.6 copy.7

commit v4 on v3

--- a/solution.py
+++ b/solution.py
@@ -77,47 +77,50 @@
         self.y, self.z, self.c = position()
         self.copies = []
 
-    def spread(self, dz):
-        y, z, c = self.y, self.z, self.c
-        zs, zr, ys, yr, ds, dr = self.sems
-        block = self.buf.at[y, (z - dz + Z) % Z, c]
+    def block(self, dy, dz, other=False):
+        y, z = (self.y - dy + Y) % Y, (self.z - dz + Z) % Z
+        c = 1 - self.c if other else self.c
+        return self.buf.at[y, z, c]
+
+    def send(self, block, send_sem, recv_sem, y, z, c):
+        self.copies.append(send(block, block, send_sem, recv_sem, at_seq((y + Y) % Y, (z + Z) % Z, c)))
+
+    def to_core(self, dy, dz):
+        ds, dr = self.sems[4:]
+        self.send(self.block(dy, dz), ds.at[dy, dz], dr.at[dy, dz], self.y, self.z, 1 - self.c)
+
+    def along_y(self, dz):
+        ys, yr = self.sems[2:4]
         for dy in (2, 1, 3):
-            self.copies.append(send(block, block, ys.at[dy, dz], yr.at[dy, dz], at_seq((y + dy) % Y, z, c)))
-        self.copies.append(send(block, block, ds.at[0, dz], dr.at[0, dz], at_seq(y, z, 1 - c)))
+            self.send(self.block(0, dz), ys.at[dy, dz], yr.at[dy, dz], self.y + dy, self.z, self.c)
 
     def start(self):
-        y, z, c = self.y, self.z, self.c
-        zs, zr, ys, yr, ds, dr = self.sems
-        own = self.buf.at[y, z, c]
+        zs, zr = self.sems[:2]
         for dz in (2, 1, 3):
-            self.copies.append(send(own, own, zs.at[dz], zr.at[dz], at_seq(y, (z + dz) % Z, c)))
-        self.spread(0)
+            self.send(self.block(0, 0), zs.at[dz], zr.at[dz], self.y, self.z + dz, self.c)
+        self.along_y(0)
+        self.to_core(0, 0)
 
     def from_z(self, dz):
-        y, z, c = self.y, self.z, self.c
-        zs, zr, ys, yr, ds, dr = self.sems
-        arrived(self.buf.at[y, (z - dz + Z) % Z, c], zs.at[dz], zr.at[dz], at_seq(y, (z - dz + Z) % Z, c))
-        self.spread(dz)
+        zs, zr = self.sems[:2]
+        arrived(self.block(0, dz), zs.at[dz], zr.at[dz], at_seq(self.y, (self.z - dz + Z) % Z, self.c))
+        self.along_y(dz)
+        self.to_core(0, dz)
 
     def from_y(self, dy, dz):
-        y, z, c = self.y, self.z, self.c
-        zs, zr, ys, yr, ds, dr = self.sems
-        block = self.buf.at[(y - dy + Y) % Y, (z - dz + Z) % Z, c]
-        arrived(block, ys.at[dy, dz], yr.at[dy, dz], at_seq((y - dy + Y) % Y, z, c))
-        self.copies.append(send(block, block, ds.at[dy, dz], dr.at[dy, dz], at_seq(y, z, 1 - c)))
+        ys, yr = self.sems[2:4]
+        arrived(self.block(dy, dz), ys.at[dy, dz], yr.at[dy, dz], at_seq((self.y - dy + Y) % Y, self.z, self.c))
+        self.to_core(dy, dz)
 
     def from_core(self, dy, dz):
-        y, z, c = self.y, self.z, self.c
-        zs, zr, ys, yr, ds, dr = self.sems
-        block = self.buf.at[(y - dy + Y) % Y, (z - dz + Z) % Z, 1 - c]
-        arrived(block, ds.at[dy, dz], dr.at[dy, dz], at_seq(y, z, 1 - c))
+        ds, dr = self.sems[4:]
+        arrived(self.block(dy, dz, other=True), ds.at[dy, dz], dr.at[dy, dz], at_seq(self.y, self.z, 1 - self.c))
 
     def finish(self):
         for copy in self.copies:
             copy.wait_send()
 
 
-ORDER = [(0, 0)] + [(0, d) for d in (1, 3, 2)] + [(dy, dz) for dz in (0, 1, 3, 2) for dy in (1, 3, 2)]
 GATHER_SEMS = [
     pltpu.SemaphoreType.DMA((Z,)), pltpu.SemaphoreType.DMA((Z,)),
     pltpu.SemaphoreType.DMA((Y, Z)), pltpu.SemaphoreType.DMA((Y, Z)),
@@ -235,10 +238,12 @@
     loads[1].wait()
     lax.fori_loop(8, 16, turn, 0)
     lax.fori_loop(0, NONE // 256, name, 0)
-    for dy, dz in ORDER[4:]:
-        gather.from_y(dy, dz)
-    for dy, dz in ORDER:
-        gather.from_core(dy, dz)
+    for dz in (0, 1, 3, 2):
+        for dy in (1, 3, 2):
+            gather.from_y(dy, dz)
+    for dz in (0, 1, 3, 2):
+        for dy in range(Y):
+            gather.from_core(dy, dz)
     gather.finish()
     load_v.wait()
 
@@ -377,11 +382,12 @@
 
         lax.fori_loop(0, Y, one, 0)
 
-    def theirs():
+    def early():
         for e in order:
             settle_all(e, other, their_acc, their_stats)
-
-    greet(seq_peers(y, z, c) + [{"head": (h + d) % GROUPS} for d in range(1, GROUPS)], theirs)
+        settle_all(order[0], c, own_acc, own_stats)
+
+    greet(seq_peers(y, z, c) + [{"head": (h + d) % GROUPS} for d in range(1, GROUPS)], early)
     copies = []
     for e in order:
         copies.append(send(their_acc.at[e], core_acc.at[e], c_send.at[e], c_recv.at[e], partner))
@@ -394,7 +400,8 @@
         rows[1:2] = total
 
     for e in order:
-        settle_all(e, c, own_acc, own_stats)
+        if e != order[0]:
+            settle_all(e, c, own_acc, own_stats)
         arrived(core_acc.at[e], c_send.at[e], c_recv.at[e], partner)
         arrived(core_stats.at[e], cs_send.at[e], cs_recv.at[e], partner)
         for d in order:
@@ -430,63 +437,73 @@
         att[y, z, c, :, i * HD : (i + 1) * HD] = turned[pl.ds(i, ROWS, stride=HEADS), :].astype(BF16)
     gather = Gather(att, *sems)
     gather.start()
+    for copy in copies:
+        copy.wait_send()
+    load_w.wait()
     near = 3 - 2 * (z % 2)
     far = Z - near
+    for dy in (1, 3):
+        gather.from_y(dy, 0)
     gather.from_z(near)
     gather.from_z(far)
-    gather.from_y(1, 0)
-    gather.from_y(3, 0)
-    gather.from_z(2)
     gather.from_y(2, 0)
-    for dy in (1, 3, 2):
-        gather.from_y(dy, near)
-    load_w.wait()
-
-    def project(pair):
+
+    def exchange(to, pair):
+        return pltpu.make_async_remote_copy(
+            src_ref=part.at[to, pair], dst_ref=parts_in.at[h, pair], send_sem=h_send.at[to, pair], recv_sem=h_recv.at[h, pair],
+            device_id={"head": to}, device_id_type=pl.DeviceIdType.MESH,
+        )
+
+    def project(dz):
+        zz = (z - dz + Z) % Z
+        pair = zz % 2
+        rows = jnp.concatenate([att[yy, zz, j] for yy in range(Y) for j in range(C)], axis=0)
+        share = dot(rows, w[...]).astype(BF16)
         for yy in range(Y):
-            to = yy * 2 + pair
-            rows = jnp.concatenate([att[yy, pair * 2 + i, j] for i in range(2) for j in range(C)], axis=0)
-            share = dot(rows, w[...]).astype(BF16)
+            to = yy * 2 + zz // 2
+            its = share[yy * C * ROWS : (yy + 1) * C * ROWS]
 
             @pl.when(to == h)
             def _():
-                parts_in[h] = share
+                parts_in[h, pair] = its
 
             @pl.when(to != h)
             def _():
-                part[to] = share
-                send(part.at[to], parts_in.at[h], h_send.at[to], h_recv.at[h], {"head": to})
-
-    for dz in (0, near):
-        for dy in (0, 1, 3, 2):
-            gather.from_core(dy, dz)
-    project(z // 2)
-    for dz in (far, 2):
+                part[to, pair] = its
+                exchange(to, pair).start()
+
+    for dy in range(Y):
+        gather.from_core(dy, 0)
+    project(0)
+    gather.from_z(2)
+    for dz in (near, far):
         for dy in (1, 3, 2):
             gather.from_y(dy, dz)
-    for dz in (far, 2):
-        for dy in (0, 1, 3, 2):
+    for dz in (near, far):
+        for dy in range(Y):
             gather.from_core(dy, dz)
-    project(1 - z // 2)
+        project(dz)
+    for dy in (1, 3, 2):
+        gather.from_y(dy, 2)
+    for dy in range(Y):
+        gather.from_core(dy, 2)
+    project(2)
+    gather.finish()
     for s in range(GROUPS):
 
         @pl.when(s != h)
         def _():
-            arrived(parts_in.at[s], h_send.at[s], h_recv.at[s], {"head": s})
-
-    out_ref[...] = sum(parts_in[s].astype(F32) for s in range(GROUPS)).astype(BF16)
+            for pair in range(2):
+                arrived(parts_in.at[s, pair], h_send.at[s, pair], h_recv.at[s, pair], {"head": s})
+
+    total = sum(parts_in[s].astype(F32) for s in range(GROUPS))
+    out_ref[...] = total.reshape(out_ref.shape).astype(BF16)
     for s in range(GROUPS):
 
         @pl.when(s != h)
         def _():
-            pltpu.make_async_remote_copy(
-                src_ref=part.at[s], dst_ref=parts_in.at[h], send_sem=h_send.at[s], recv_sem=h_recv.at[h],
-                device_id={"head": s}, device_id_type=pl.DeviceIdType.MESH,
-            ).wait_send()
-
-    gather.finish()
-    for copy in copies:
-        copy.wait_send()
+            for pair in range(2):
+                exchange(s, pair).wait_send()
 
 
 def finish(pick, found, w):
@@ -510,12 +527,12 @@
             VMEM((TILE, HD), F32),
             VMEM((Y, Z, C, ROWS, HEADS * HD), BF16),
             VMEM((HEADS * HD, width), BF16),
-            VMEM((GROUPS, rows, width), BF16), VMEM((GROUPS, rows, width), BF16),
+            VMEM((GROUPS, 2, rows // 2, width), BF16), VMEM((GROUPS, 2, rows // 2, width), BF16),
             dma,
             *[dma((Z,)) for _ in range(4)],
             *[dma((Y, Z)) for _ in range(4)],
             *[dma((Z,)) for _ in range(4)],
-            dma((GROUPS,)), dma((GROUPS,)),
+            dma((GROUPS, 2)), dma((GROUPS, 2)),
             *GATHER_SEMS,
         ],
         compiler_params=pltpu.CompilerParams(collective_id=1, has_side_effects=True, vmem_limit_bytes=12 << 20),

time: 64.6 us -> 64.1 us (level); the launches traced: 64.8 us -> 63.3 us
  Pallas kernels: 64.2 us -> 62.7 us
    pallas_call x1, Pallas kernels: 37.1 us -> 35.7 us  [finish(): pl.pallas_call(finish_kernel, out_shape=jax.ShapeDtypeStruct((rows, width...]
where the time goes in v4:
time: 64.1 us; the launch traced here: 63.3 us
  Pallas kernels  62.7 us (98%)
    pallas_call x1, Pallas kernels, finish(): pl.pallas_call(finish_kernel, out_shape=jax.ShapeDtypeStruct((rows, width...  35.7 us
    pallas_call x1, Pallas kernels, prepare(): pl.pallas_call(prepare_kernel, out_shape=(jax.ShapeDtypeStruct((Y, Z, C,...  19.8 us
    pallas_call x1, Pallas kernels, attend(): pl.pallas_call(attend_kernel, out_shape=VMEM((NONE + 8, 2, HEADS, HD), F3...  7.23 us

profile of v4, /device:TPU:33, one launch (start us, length us, event | category | flops | bytes accessed | tf_op | source)
XLA Modules:
  0.0 63.3 jit_solution(10190996336978253200)
XLA Ops:
  0.0 19.8 %prepare.1 = (bf16[4,4,2,128,128]{4,3,2,1,0:T(8,128)(2,1)S(1)}, s32[32,128]{1,0:T(8,128)S(1)}, s32[40,128]{1,0:T(8,128)S(1)}, bf16[64,128,128]{2,1,0:T(8,128)(2,1)S(1)}, bf16[64,128,128]{2,1,0:T(8,128)(2,1)S(1)}) custom-call(bf16[128,128]{1,0:T(8,128)(2,1)} %bitcast.8, s32[64,512]{1,0:T(8,128)} %bitcast.7, s32[1,512]{1,0:T(1,128)} %bitcast.9, ...), custom_call_target="tpu_custom_call" | custom-call | tf_op jit(solution)/shard_map/prepare/pallas_call | solution.py:254
  19.8 7.2 %attend.1.found = f32[2568,2,8,128]{3,2,1,0:T(8,128)S(1)} custom-call(s32[32,128]{1,0:T(8,128)S(1)} %get-tuple-element.10.pick, s32[40,128]{1,0:T(8,128)S(1)} %get-tuple-element.11.who, bf16[32,128,128]{2,1,0:T(8,128)(2,1)S(1)} %bitcast.5, bf16[64,128,128]{2,1,0:T(8,128)(2,1)S(1)} %get-tuple-element.13.kt, bf16[64,128,128]{2,1,0:T(8,128)(2,1)S(1)} %get-tuple-element.14.v), custom_call_target="tpu_custom_call" | custom-call | tf_op jit(solution)/shard_map/attend/pallas_call | solution.py:321
  27.0 35.7 %finish.1 = bf16[64,256]{1,0:T(8,128)(2,1)S(1)} custom-call(s32[32,128]{1,0:T(8,128)S(1)} %get-tuple-element.10.pick, f32[2568,2,8,128]{3,2,1,0:T(8,128)S(1)} %attend.1.found, bf16[1024,256]{1,0:T(8,128)(2,1)} %w_ref.1), custom_call_target="tpu_custom_call" | custom-call | tf_op jit(solution)/shard_map/finish/pallas_call | solution.py:514
  62.7 0.6 copy.7

commit v5 on v4

--- a/solution.py
+++ b/solution.py
@@ -56,8 +56,8 @@
 
 
 def seq_peers(y, z, c):
-    peers = [at_seq(y, z, 1 - c)]
-    peers += [at_seq(y, (z + d) % Z, c) for d in range(1, Z)]
+    peers = [at_seq(y, (z + d) % Z, c) for d in (2, 1, 3)]
+    peers += [at_seq(y, z, 1 - c)]
     peers += [at_seq((y + d) % Y, z, c) for d in range(1, Y)]
     return peers
 
@@ -277,7 +277,11 @@
     )(q, table, counts, cache)
 
 
-def attend_kernel(pick, who, q_in, kt, v, found, q, scores):
+def attend_kernel(pick_in, who_in, q_in, kt, v, found, q, scores, pick, who, sems):
+    tables = [pltpu.make_async_copy(pick_in, pick, sems.at[0]), pltpu.make_async_copy(who_in, who, sems.at[1])]
+    for table in tables:
+        table.start()
+
     def widen(i, carry):
         for j in range(4):
             q[pl.ds((i * 4 + j) * ROWS, ROWS)] = q_in[i * 4 + j].astype(F32).reshape(ROWS, HEADS, HD)
@@ -287,6 +291,8 @@
     found[pl.ds(NONE, 8), 0] = jnp.zeros((8, HEADS, HD), F32)
     found[pl.ds(NONE, 8), 1] = jnp.full((8, HEADS, HD), -1e30, F32)
     ones = jnp.ones((PAGE, HD), BF16)
+    for table in tables:
+        table.wait()
 
     def scores_of(g):
         for u in range(UNROLL):
@@ -317,15 +323,17 @@
 
 def attend(pick, who, q, kt, v):
     vmem = pl.BlockSpec(memory_space=VMEM)
-    smem = pl.BlockSpec(memory_space=pltpu.SMEM)
     return pl.pallas_call(
         attend_kernel,
         out_shape=VMEM((NONE + 8, 2, HEADS, HD), F32),
-        in_specs=[smem, smem, vmem, vmem, vmem],
+        in_specs=[vmem] * 5,
         out_specs=vmem,
         scratch_shapes=[
             VMEM((BATCH, HEADS, HD), F32),
             VMEM((UNROLL, CHUNK * HEADS, PAGE), F32),
+            pltpu.SMEM((BLOCKS, 128), jnp.int32),
+            pltpu.SMEM((STEPS, 128), jnp.int32),
+            pltpu.SemaphoreType.DMA((2,)),
         ],
         compiler_params=pltpu.CompilerParams(vmem_limit_bytes=8 << 20),
         name="attend",

time: 64.1 us -> 63.9 us (level)
  no operation moved by 1% of the time
where the time goes in v5:
time: 63.9 us; the launch traced here: 63.1 us
  Pallas kernels  62.4 us (98%)
    pallas_call x1, Pallas kernels, finish(): pl.pallas_call(finish_kernel, out_shape=jax.ShapeDtypeStruct((rows, width...  35.5 us
    pallas_call x1, Pallas kernels, prepare(): pl.pallas_call(prepare_kernel, out_shape=(jax.ShapeDtypeStruct((Y, Z, C,...  19.8 us
    pallas_call x1, Pallas kernels, attend(): pl.pallas_call(attend_kernel, out_shape=VMEM((NONE + 8, 2, HEADS, HD), F3...  7.1 us

profile of v5, /device:TPU:33, one launch (start us, length us, event | category | flops | bytes accessed | tf_op | source)
XLA Modules:
  0.0 63.1 jit_solution(17844506948547402186)
XLA Ops:
  0.0 19.8 %prepare.1 = (bf16[4,4,2,128,128]{4,3,2,1,0:T(8,128)(2,1)S(1)}, s32[32,128]{1,0:T(8,128)S(1)}, s32[40,128]{1,0:T(8,128)S(1)}, bf16[64,128,128]{2,1,0:T(8,128)(2,1)S(1)}, bf16[64,128,128]{2,1,0:T(8,128)(2,1)S(1)}) custom-call(bf16[128,128]{1,0:T(8,128)(2,1)} %bitcast.8, s32[64,512]{1,0:T(8,128)} %bitcast.7, s32[1,512]{1,0:T(1,128)} %bitcast.9, ...), custom_call_target="tpu_custom_call" | custom-call | tf_op jit(solution)/shard_map/prepare/pallas_call | solution.py:254
  19.8 7.1 %attend.1.found = f32[2568,2,8,128]{3,2,1,0:T(8,128)S(1)} custom-call(s32[32,128]{1,0:T(8,128)S(1)} %get-tuple-element.10.pick_in.pick, s32[40,128]{1,0:T(8,128)S(1)} %get-tuple-element.11.who_in, bf16[32,128,128]{2,1,0:T(8,128)(2,1)S(1)} %bitcast.5, bf16[64,128,128]{2,1,0:T(8,128)(2,1)S(1)} %get-tuple-element.13.kt, ...), custom_call_target="tpu_custom_call" | custom-call | tf_op jit(solution)/shard_map/attend/pallas_call | solution.py:326
  26.9 35.5 %finish.1 = bf16[64,256]{1,0:T(8,128)(2,1)S(1)} custom-call(s32[32,128]{1,0:T(8,128)S(1)} %get-tuple-element.10.pick_in.pick, f32[2568,2,8,128]{3,2,1,0:T(8,128)S(1)} %attend.1.found, bf16[1024,256]{1,0:T(8,128)(2,1)} %w_ref.1), custom_call_target="tpu_custom_call" | custom-call | tf_op jit(solution)/shard_map/finish/pallas_call | solution.py:522
  62.5 0.6 copy.7

commit v6 on v5

--- a/solution.py
+++ b/solution.py
@@ -241,10 +241,10 @@
     for dz in (0, 1, 3, 2):
         for dy in (1, 3, 2):
             gather.from_y(dy, dz)
+    gather.finish()
     for dz in (0, 1, 3, 2):
         for dy in range(Y):
             gather.from_core(dy, dz)
-    gather.finish()
     load_v.wait()
 
 
@@ -480,19 +480,21 @@
                 part[to, pair] = its
                 exchange(to, pair).start()
 
+    gather.from_z(2)
     for dy in range(Y):
         gather.from_core(dy, 0)
     project(0)
-    gather.from_z(2)
     for dz in (near, far):
         for dy in (1, 3, 2):
             gather.from_y(dy, dz)
-    for dz in (near, far):
-        for dy in range(Y):
-            gather.from_core(dy, dz)
-        project(dz)
+    for dy in range(Y):
+        gather.from_core(dy, near)
+    project(near)
     for dy in (1, 3, 2):
         gather.from_y(dy, 2)
+    for dy in range(Y):
+        gather.from_core(dy, far)
+    project(far)
     for dy in range(Y):
         gather.from_core(dy, 2)
     project(2)

time: 63.9 us -> 63.7 us (level); the launches traced: 63.1 us -> 63.8 us
  Pallas kernels: 62.4 us -> 63.1 us
where the time goes in v6:
time: 63.7 us; the launch traced here: 63.8 us
  Pallas kernels  63.1 us (99%)
    pallas_call x1, Pallas kernels, finish(): pl.pallas_call(finish_kernel, out_shape=jax.ShapeDtypeStruct((rows, width...  35.9 us
    pallas_call x1, Pallas kernels, prepare(): pl.pallas_call(prepare_kernel, out_shape=(jax.ShapeDtypeStruct((Y, Z, C,...  19.7 us
    pallas_call x1, Pallas kernels, attend(): pl.pallas_call(attend_kernel, out_shape=VMEM((NONE + 8, 2, HEADS, HD), F3...  7.46 us

profile of v6, /device:TPU:33, one launch (start us, length us, event | category | flops | bytes accessed | tf_op | source)
XLA Modules:
  0.0 63.8 jit_solution(1784911568276010802)
XLA Ops:
  0.0 19.7 %prepare.1 = (bf16[4,4,2,128,128]{4,3,2,1,0:T(8,128)(2,1)S(1)}, s32[32,128]{1,0:T(8,128)S(1)}, s32[40,128]{1,0:T(8,128)S(1)}, bf16[64,128,128]{2,1,0:T(8,128)(2,1)S(1)}, bf16[64,128,128]{2,1,0:T(8,128)(2,1)S(1)}) custom-call(bf16[128,128]{1,0:T(8,128)(2,1)} %bitcast.8, s32[64,512]{1,0:T(8,128)} %bitcast.7, s32[1,512]{1,0:T(1,128)} %bitcast.9, ...), custom_call_target="tpu_custom_call" | custom-call | tf_op jit(solution)/shard_map/prepare/pallas_call | solution.py:254
  19.7 7.5 %attend.1.found = f32[2568,2,8,128]{3,2,1,0:T(8,128)S(1)} custom-call(s32[32,128]{1,0:T(8,128)S(1)} %get-tuple-element.10.pick_in.pick, s32[40,128]{1,0:T(8,128)S(1)} %get-tuple-element.11.who_in, bf16[32,128,128]{2,1,0:T(8,128)(2,1)S(1)} %bitcast.5, bf16[64,128,128]{2,1,0:T(8,128)(2,1)S(1)} %get-tuple-element.13.kt, ...), custom_call_target="tpu_custom_call" | custom-call | tf_op jit(solution)/shard_map/attend/pallas_call | solution.py:326
  27.2 35.9 %finish.1 = bf16[64,256]{1,0:T(8,128)(2,1)S(1)} custom-call(s32[32,128]{1,0:T(8,128)S(1)} %get-tuple-element.10.pick_in.pick, f32[2568,2,8,128]{3,2,1,0:T(8,128)S(1)} %attend.1.found, bf16[1024,256]{1,0:T(8,128)(2,1)} %w_ref.1), custom_call_target="tpu_custom_call" | custom-call | tf_op jit(solution)/shard_map/finish/pallas_call | solution.py:524
  63.1 0.6 copy.7
